TPU v7x, 32 devices: a whole 2x2x4 slice. The times are simulated.
32 devices in a mesh: groups: 2 (over y), blk: 16 (over z, x, core).
Axes of the slice: x: 2, y: 2, z: 4, core: 2. Of those that a mesh axis runs over, the one named last changes fastest.
Arguments:
- current_states: float32 [16, 8192], P(None, ('groups', 'blk')), parts along dimension 1, may hold values from -0.5 to 0.5
- next_states: float32 [16, 8192], P(None, ('groups', 'blk')), parts along dimension 1, may hold values from -1 to 1
- next_values: float32 [8192], P(('groups', 'blk')), parts along dimension 0, may hold values from 0 to 2.5
- vol_table: float32 [12, 16], replicated, may hold values from 0.15 to 0.45
- date_index: int32 [1], replicated, may hold values from 0 to 11
- strike: float32 [1], replicated, may hold values from 0.8 to 1.2
Outputs:
- continuation: float32 [8192], P(('groups', 'blk')), parts along dimension 0
- node_value: float32 [8192], P(('groups', 'blk')), parts along dimension 0
There are 2 independent parts, one for each index of `groups`. A program takes and returns all parts, laid end to end along the dimension named above; an argument that names none is the same for every part. Nothing has to cross between parts.
All inputs are finite; a program needn't handle non-finite values.
Results may differ from a plain program's by a relative error of at most 0.00012.
Values sent between devices are 32-bit elements; how exact they have to be, the bound alone decides.
No kernel may reach another device: no remote copies, remote signals or barrier semaphores. Data moves between devices by JAX's collectives and lax.ppermute only.
A program may use at most 64 MiB of HBM per device.

v0:
```python
import math

import jax
import jax.numpy as jnp
from jax import lax
from jax.sharding import PartitionSpec as P

rate_year = 0.05
step_years = 0.1


def scaled_states(current_states, next_states, vol_table, date_index):
    date_count = vol_table.shape[0]
    picked = (jnp.arange(date_count, dtype=jnp.int32) == date_index[0]).astype(jnp.float32)
    vol_row = jnp.sum(vol_table * picked[:, None], axis=0)
    spread = vol_row * math.sqrt(step_years)
    drift_term = (rate_year - 0.5 * vol_row * vol_row) * step_years
    anchor = (current_states + drift_term[:, None]) / spread[:, None]
    target = next_states / spread[:, None]
    anchor_half = 0.5 * jnp.sum(anchor * anchor, axis=0, keepdims=True)
    target_half = 0.5 * jnp.sum(target * target, axis=0, keepdims=True)
    return (anchor, anchor_half, target, target_half)


def kernel_block(source_states, source_norms, sink_states, sink_norms):
    inner_term = lax.dot_general(
        source_states,
        sink_states,
        (((0,), (0,)), ((), ())),
        precision=lax.Precision.HIGHEST,
        preferred_element_type=jnp.float32,
    )
    return jnp.exp(inner_term - source_norms.reshape(-1, 1) - sink_norms)


def block_rows(row_count):
    if row_count <= 4096:
        return row_count
    return math.gcd(row_count, 4096)


def finish(current_states, totals, strike):
    continuation = math.exp(-rate_year * step_years) * totals[0] / totals[1]
    payoff = jnp.maximum(jnp.max(jnp.exp(current_states), axis=0) - strike[0], 0.0)
    return (continuation, jnp.maximum(payoff, continuation))


def body(current_states, next_states, next_values, vol_table, date_index, strike):
    anchor, anchor_half, target, target_half = scaled_states(
        current_states, next_states, vol_table, date_index
    )
    local_count = anchor.shape[1]
    pieces = (
        lax.all_gather(anchor, "blk", axis=1, tiled=True),
        lax.all_gather(anchor_half, "blk", axis=1, tiled=True),
    )
    row_count = pieces[0].shape[1]
    block_size = block_rows(row_count)

    def one_block(number, inner_sum):
        source_part = lax.dynamic_slice_in_dim(pieces[0], number * block_size, block_size, 1)
        norm_part = lax.dynamic_slice_in_dim(pieces[1], number * block_size, block_size, 1)
        return inner_sum + jnp.sum(
            kernel_block(source_part, norm_part, target, target_half), axis=0
        )

    density = lax.fori_loop(
        0, row_count // block_size, one_block, jnp.zeros((local_count,), jnp.float32)
    )
    extras = jnp.concatenate(
        [target_half, (next_values / density)[None, :], (1.0 / density)[None, :]], axis=0
    )
    add_pieces = (
        lax.all_gather(target, "blk", axis=1, tiled=True),
        lax.all_gather(extras, "blk", axis=1, tiled=True),
    )
    row_count = add_pieces[0].shape[1]
    add_block_size = block_rows(row_count)

    def one_block(number, inner_sum):
        sink_part = lax.dynamic_slice_in_dim(
            add_pieces[0], number * add_block_size, add_block_size, 1
        )
        extra_part = lax.dynamic_slice_in_dim(
            add_pieces[1], number * add_block_size, add_block_size, 1
        )
        weights = kernel_block(sink_part, extra_part[0:1], anchor, anchor_half)
        return inner_sum + jnp.dot(
            extra_part[1:3],
            weights,
            precision=lax.Precision.HIGHEST,
            preferred_element_type=jnp.float32,
        )

    totals = lax.fori_loop(
        0, row_count // add_block_size, one_block, jnp.zeros((2, local_count), jnp.float32)
    )
    return finish(current_states, totals, strike)


def solution(mesh):
    placed = (
        P(None, ("groups", "blk")),
        P(None, ("groups", "blk")),
        P(("groups", "blk")),
        P(),
        P(),
        P(),
    )
    return jax.shard_map(
        body,
        mesh=mesh,
        in_specs=placed,
        out_specs=(P(("groups", "blk")), P(("groups", "blk"))),
        check_vma=False,
    )
```

profile of v0, /device:TPU:0, one launch (start us, length us, event | category | flops | bytes accessed | tf_op | source)
XLA Modules:
  0.0 93.4 jit_solution(17060757897564297539)
XLA Ops:
  0.6 0.0 copy-start.1
  1.3 0.8 multiply_reduce_fusion.2
  2.1 0.8 multiply_reduce_fusion
  2.9 23.8 %all_gather.12 = f32[16,4096]{1,0:T(8,128)S(1)} all-gather(f32[16,256]{1,0:T(8,128)S(1)} %get-tuple-element.33), channel_id=1, replica_groups=mesh['groups'=2,'blk'=16] {'blk'}, dimensions={1}, use_global_device_ids=true | all-gather | bytes 278528 | tf_op jit(solution)/shard_map/all_gather | solution.py:54
  26.7 17.5 %all-gather.1 = f32[16,1,256]{2,1,0:T(1,128)S(1)} all-gather(f32[1,1,256]{2,1,0:T(1,128)S(1)} %bitcast.18), channel_id=2, replica_groups=mesh['groups'=2,'blk'=16] {'blk'}, dimensions={0}, use_global_device_ids=true | all-gather | bytes 17408 | tf_op jit(solution)/shard_map/all_gather | solution.py:55
  44.2 4.4 %fusion.4 = f32[256]{0:T(256)S(1)} fusion(f32[256]{0:T(256)S(1)} %broadcast_multiply_fusion.1, f32[4096]{0:T(1024)S(1)} %bitcast.17, f32[16,4096]{1,0:T(8,128)S(1)} %all_gather.12, f32[16,256]{1,0:T(8,128)S(1)} %get-tuple-element.45), kind=kOutput, calls=%fused_computation.6 | convolution fusion | flops 204472064 | bytes 296960 | tf_op jit(solution)/shard_map/while/body/eval_jaxpr/dot_general | solution.py:26
  48.6 0.0 copy-done.1
  48.7 18.9 %all_gather.14 = f32[3,4096]{1,0:T(4,128)S(1)} all-gather(f32[3,256]{1,0:T(4,128)S(1)} %pad_maximum_fusion), channel_id=1, replica_groups=mesh['groups'=2,'blk'=16] {'blk'}, dimensions={1}, use_global_device_ids=true | all-gather | bytes 52224 | tf_op jit(solution)/shard_map/all_gather | solution.py:75
  67.6 18.2 %all_gather.15 = f32[16,4096]{1,0:T(8,128)S(1)} all-gather(f32[16,256]{1,0:T(8,128)S(1)} %get-tuple-element.45), channel_id=1, replica_groups=mesh['groups'=2,'blk'=16] {'blk'}, dimensions={1}, use_global_device_ids=true | all-gather | bytes 278528 | tf_op jit(solution)/shard_map/all_gather | solution.py:74
  85.8 4.6 %fusion.1 = f32[4096,256]{1,0:T(8,128)S(1)} fusion(f32[16,4096]{1,0:T(8,128)S(1)} %all_gather.15, f32[16,256]{1,0:T(8,128)S(1)} %get-tuple-element.33, f32[256]{0:T(256)S(1)} %broadcast_multiply_fusion, f32[4096]{0:T(1024)S(1)} %bitcast.16), kind=kOutput, calls=%fused_computation.2 | convolution fusion | flops 203423744 | bytes 4490240 | tf_op jit(solution)/shard_map/while/body/eval_jaxpr/dot_general | solution.py:26
  90.4 1.7 %fusion.5 = f32[2,256]{1,0:T(2,128)S(1)} fusion(f32[4096,256]{1,0:T(8,128)S(1)} %fusion.1, f32[3,4096]{1,0:T(4,128)S(1)} %all_gather.14), kind=kOutput, calls=%fused_computation.7 | convolution fusion | flops 25165824 | bytes 4229120 | tf_op jit(solution)/shard_map/while/body/eval_jaxpr/dot_general | solution.py:88
  92.2 0.0 copy-start
  92.8 0.6 maximum_maximum_fusion
  93.4 0.0 copy-done
  (8 shorter events, 0.1 us)
Async XLA Ops:
  0.6 48.0 %copy-start.1 = (f32[256]{0:T(256)S(1)}, f32[256]{0:T(256)}, u32[]{:S(2)}) copy-start(f32[256]{0:T(256)} %param.8) | copy-start | bytes 3076
  92.2 1.2 %copy-start = (f32[1,256]{1,0:T(1,128)}, f32[1,256]{1,0:T(1,128)S(1)}, u32[]{:S(2)}) copy-start(f32[1,256]{1,0:T(1,128)S(1)} %slice_divide_fusion) | copy-start | bytes 3076
where the time goes:
time: 93.8 us; the launch traced here: 93.4 us
  blocking collectives  78.4 us (84%)
  matrix products  10.8 us (12%)
  other arithmetic  2.22 us (2%)
  between operations  2.02 us (2%)
    all_gather x1, blocking collectives, body(): lax.all_gather(anchor, 'blk', axis=1, tiled=True)  23.8 us
    all_gather x1, blocking collectives, body(): lax.all_gather(extras, 'blk', axis=1, tiled=True)  18.9 us
    all_gather x1, blocking collectives, body(): lax.all_gather(target, 'blk', axis=1, tiled=True)  18.2 us
    all_gather x1, blocking collectives, body(): lax.all_gather(anchor_half, 'blk', axis=1, tiled=True)  17.5 us
    dot_general x2, matrix products, kernel_block(): lax.dot_general(source_states, sink_states, (((0,), (0,)), ((), ())), pre...  9.04 us

commit v1 on v0

--- a/solution.py
+++ b/solution.py
@@ -1,12 +1,20 @@
+import functools
 import math
 
 import jax
 import jax.numpy as jnp
 from jax import lax
+from jax.experimental import pallas as pl
+from jax.experimental.pallas import tpu as pltpu
 from jax.sharding import PartitionSpec as P
 
 rate_year = 0.05
 step_years = 0.1
+log2_e = math.log2(math.e)
+lane_tile = 512
+row_tile = 256
+depth = 128
+doubling_limit = 32
 
 
 def scaled_states(current_states, next_states, vol_table, date_index):
@@ -45,7 +53,7 @@
     return (continuation, jnp.maximum(payoff, continuation))
 
 
-def body(current_states, next_states, next_values, vol_table, date_index, strike):
+def gathered_body(current_states, next_states, next_values, vol_table, date_index, strike):
     anchor, anchor_half, target, target_half = scaled_states(
         current_states, next_states, vol_table, date_index
     )
@@ -57,7 +65,7 @@
     row_count = pieces[0].shape[1]
     block_size = block_rows(row_count)
 
-    def one_block(number, inner_sum):
+    def density_block(number, inner_sum):
         source_part = lax.dynamic_slice_in_dim(pieces[0], number * block_size, block_size, 1)
         norm_part = lax.dynamic_slice_in_dim(pieces[1], number * block_size, block_size, 1)
         return inner_sum + jnp.sum(
@@ -65,7 +73,7 @@
         )
 
     density = lax.fori_loop(
-        0, row_count // block_size, one_block, jnp.zeros((local_count,), jnp.float32)
+        0, row_count // block_size, density_block, jnp.zeros((local_count,), jnp.float32)
     )
     extras = jnp.concatenate(
         [target_half, (next_values / density)[None, :], (1.0 / density)[None, :]], axis=0
@@ -74,16 +82,10 @@
         lax.all_gather(target, "blk", axis=1, tiled=True),
         lax.all_gather(extras, "blk", axis=1, tiled=True),
     )
-    row_count = add_pieces[0].shape[1]
-    add_block_size = block_rows(row_count)
-
-    def one_block(number, inner_sum):
-        sink_part = lax.dynamic_slice_in_dim(
-            add_pieces[0], number * add_block_size, add_block_size, 1
-        )
-        extra_part = lax.dynamic_slice_in_dim(
-            add_pieces[1], number * add_block_size, add_block_size, 1
-        )
+
+    def weighted_block(number, inner_sum):
+        sink_part = lax.dynamic_slice_in_dim(add_pieces[0], number * block_size, block_size, 1)
+        extra_part = lax.dynamic_slice_in_dim(add_pieces[1], number * block_size, block_size, 1)
         weights = kernel_block(sink_part, extra_part[0:1], anchor, anchor_half)
         return inner_sum + jnp.dot(
             extra_part[1:3],
@@ -93,12 +95,210 @@
         )
 
     totals = lax.fori_loop(
-        0, row_count // add_block_size, one_block, jnp.zeros((2, local_count), jnp.float32)
+        0, row_count // block_size, weighted_block, jnp.zeros((2, local_count), jnp.float32)
     )
     return finish(current_states, totals, strike)
 
 
+def spread_columns(vol_ref, index_ref):
+    dates, assets = vol_ref.shape
+    rows = lax.broadcasted_iota(jnp.int32, (dates, assets), 0)
+    vol_row = jnp.sum(jnp.where(rows == index_ref[0], vol_ref[...], 0.0), axis=0, keepdims=True)
+    square = (assets, assets)
+    diagonal = lax.broadcasted_iota(jnp.int32, square, 0) == lax.broadcasted_iota(
+        jnp.int32, square, 1
+    )
+    vol = jnp.sum(
+        jnp.where(diagonal, jnp.broadcast_to(vol_row, square), 0.0), axis=1, keepdims=True
+    )
+    spread = vol * math.sqrt(step_years)
+    drift_term = (rate_year - 0.5 * vol * vol) * step_years
+    return 1.0 / spread, drift_term
+
+
+def in_three(x):
+    first = x.astype(jnp.bfloat16)
+    rest = x - first.astype(jnp.float32)
+    second = rest.astype(jnp.bfloat16)
+    third = (rest - second.astype(jnp.float32)).astype(jnp.bfloat16)
+    return first, second, third
+
+
+def with_norm(pieces, norm, ones_first):
+    rows = lax.broadcasted_iota(jnp.int32, (16, norm.shape[1]), 0)
+    shift = 3 if ones_first else 0
+    tile = jnp.where((rows >= 3 - shift) & (rows < 6 - shift), 1.0, 0.0)
+    for k, part in enumerate(in_three(norm)):
+        tile = jnp.where(rows == k + shift, part.astype(jnp.float32), tile)
+    return jnp.concatenate(list(pieces) + [tile.astype(jnp.bfloat16)], axis=0)
+
+
+def source_operand(states, inverse, drift_term):
+    anchor = (states + drift_term) * inverse
+    half = (0.5 * log2_e) * jnp.sum(anchor * anchor, axis=0, keepdims=True)
+    a1, a2, a3 = in_three(anchor * log2_e)
+    stacked = with_norm((a1, a1, a2, a1, a2, a3), -half, False)
+    fill = jnp.zeros((depth - stacked.shape[0], stacked.shape[1]), jnp.bfloat16)
+    return jnp.concatenate([stacked, fill], axis=0).T
+
+
+def sink_operand(states, inverse):
+    target = states * inverse
+    half = (0.5 * log2_e) * jnp.sum(target * target, axis=0, keepdims=True)
+    t1, t2, t3 = in_three(target)
+    stacked = with_norm((t1, t2, t1, t3, t2, t1), -half, True)
+    fill = jnp.zeros((depth - stacked.shape[0], stacked.shape[1]), jnp.bfloat16)
+    return jnp.concatenate([stacked, fill], axis=0)
+
+
+def partial_density(left_ref, right_ref, density_ref):
+    source_count, sink_count = left_ref.shape[0], right_ref.shape[1]
+    width = math.gcd(sink_count, lane_tile)
+    height = math.gcd(source_count, row_tile)
+
+    def columns(number, carry):
+        part = pl.ds(pl.multiple_of(number * width, width), width)
+        right = right_ref[:, part]
+        total = jnp.zeros((8, width), jnp.float32)
+        for k in range(source_count // height):
+            exponent = jnp.dot(
+                left_ref[k * height : (k + 1) * height, :],
+                right,
+                preferred_element_type=jnp.float32,
+            )
+            total += jnp.sum(jnp.exp2(exponent).reshape(height // 8, 8, width), axis=0)
+        density_ref[:, part] = jnp.sum(total, axis=0, keepdims=True)
+        return carry
+
+    lax.fori_loop(0, sink_count // width, columns, 0)
+
+
+def own_kernel(assets, index_ref, vol_ref, blocks_ref, left_ref, right_ref, density_ref):
+    inverse, drift_term = spread_columns(vol_ref, index_ref)
+    count = blocks_ref.shape[2]
+    for b in range(blocks_ref.shape[0]):
+        part = slice(b * count, (b + 1) * count)
+        left_ref[part, :] = source_operand(blocks_ref[b, 0:assets, :], inverse, drift_term)
+        right_ref[:, part] = sink_operand(blocks_ref[b, assets : 2 * assets, :], inverse)
+    partial_density(left_ref, right_ref, density_ref)
+
+
+def other_kernel(assets, index_ref, vol_ref, blocks_ref, left_ref, right_ref, density_ref):
+    inverse, _ = spread_columns(vol_ref, index_ref)
+    count = blocks_ref.shape[2]
+    for b in range(blocks_ref.shape[0]):
+        part = slice(b * count, (b + 1) * count)
+        right_ref[:, part] = sink_operand(blocks_ref[b, 0:assets, :], inverse)
+    partial_density(left_ref, right_ref, density_ref)
+
+
+def weight_kernel(
+    assets,
+    strike_ref,
+    blocks_ref,
+    others_ref,
+    left_ref,
+    right_ref,
+    other_right_ref,
+    density_ref,
+    received_ref,
+    continuation_ref,
+    node_ref,
+    ratio_ref,
+):
+    block_count, _, count = blocks_ref.shape
+    half = block_count * count
+    for k, (values_ref, row) in enumerate(((blocks_ref, 2 * assets), (others_ref, assets))):
+        inverse = 1.0 / (density_ref[k : k + 1, :] + received_ref[1 - k : 2 - k, :])
+        ratio_ref[1:2, k * half : (k + 1) * half] = inverse
+        for b in range(block_count):
+            part = slice(b * count, (b + 1) * count)
+            ratio_ref[0:1, k * half + b * count : k * half + (b + 1) * count] = (
+                values_ref[b, row : row + 1, :] * inverse[:, part]
+            )
+    width = math.gcd(half, lane_tile)
+    left = left_ref[...]
+    weighted = jnp.zeros((count, 128), jnp.float32)
+    mass = jnp.zeros((count, 128), jnp.float32)
+    for k, operand_ref in enumerate((right_ref, other_right_ref)):
+        for number in range(half // width):
+            weights = jnp.exp2(
+                jnp.dot(
+                    left,
+                    operand_ref[:, number * width : (number + 1) * width],
+                    preferred_element_type=jnp.float32,
+                )
+            )
+            for lane in range(0, width, 128):
+                place = k * half + number * width + lane
+                piece = weights[:, lane : lane + 128]
+                weighted += piece * ratio_ref[0:1, place : place + 128]
+                mass += piece * ratio_ref[1:2, place : place + 128]
+    weighted_row = jnp.sum(weighted.T, axis=0, keepdims=True)
+    mass_row = jnp.sum(mass.T, axis=0, keepdims=True)
+    continuation = math.exp(-rate_year * step_years) * weighted_row / mass_row
+    best = jnp.max(jnp.exp(blocks_ref[0, 0:assets, :]), axis=0, keepdims=True)
+    payoff = jnp.maximum(best - strike_ref[0], 0.0)
+    continuation_ref[...] = continuation
+    node_ref[...] = jnp.maximum(payoff, continuation)
+
+
+smem = pl.BlockSpec(memory_space=pltpu.SMEM)
+vmem = pl.BlockSpec(memory_space=pltpu.VMEM)
+
+
+def doubled_body(blk_size, current_states, next_states, next_values, vol_table, date_index, strike):
+    assets, count = current_states.shape
+
+    def across(array, mask):
+        return lax.ppermute(array, "blk", [(i, i ^ mask) for i in range(blk_size)])
+
+    blocks = jnp.concatenate([current_states, next_states, next_values[None, :]], axis=0)[None]
+    mask = blk_size // 2
+    while mask > 1:
+        blocks = jnp.concatenate([blocks, across(blocks, mask)], axis=0)
+        mask //= 2
+    others = across(blocks[:, assets:, :], 1)
+    half = blocks.shape[0] * count
+    left_shape = jax.ShapeDtypeStruct((half, depth), jnp.bfloat16)
+    right_shape = jax.ShapeDtypeStruct((depth, half), jnp.bfloat16)
+    density_shape = jax.ShapeDtypeStruct((1, half), jnp.float32)
+    cost = pl.CostEstimate(
+        flops=2 * depth * half * half, transcendentals=half * half, bytes_accessed=0
+    )
+    left, right, own_density = pl.pallas_call(
+        functools.partial(own_kernel, assets),
+        out_shape=(left_shape, right_shape, density_shape),
+        in_specs=[smem, vmem, vmem],
+        out_specs=(vmem, vmem, vmem),
+        cost_estimate=cost,
+        name="own_density",
+    )(date_index, vol_table, blocks)
+    other_right, other_density = pl.pallas_call(
+        functools.partial(other_kernel, assets),
+        out_shape=(right_shape, density_shape),
+        in_specs=[smem, vmem, vmem, vmem],
+        out_specs=(vmem, vmem),
+        cost_estimate=cost,
+        name="other_density",
+    )(date_index, vol_table, others, left)
+    density = jnp.concatenate([own_density, other_density], axis=0)
+    received = across(density, 1)
+    row_shape = jax.ShapeDtypeStruct((1, count), jnp.float32)
+    continuation, node_value = pl.pallas_call(
+        functools.partial(weight_kernel, assets),
+        grid=(1,),
+        out_shape=(row_shape, row_shape),
+        in_specs=[smem, vmem, vmem, pl.BlockSpec((count, depth), lambda i: (0, 0)), vmem, vmem, vmem, vmem],
+        out_specs=(vmem, vmem),
+        scratch_shapes=[pltpu.VMEM((2, 2 * half), jnp.float32)],
+        name="weights",
+    )(strike, blocks, others, left, right, other_right, density, received)
+    return continuation.reshape(count), node_value.reshape(count)
+
+
 def solution(mesh):
+    blk_size = mesh.shape["blk"]
     placed = (
         P(None, ("groups", "blk")),
         P(None, ("groups", "blk")),
@@ -107,8 +307,9 @@
         P(),
         P(),
     )
+    doubled = 2 <= blk_size <= doubling_limit and blk_size & (blk_size - 1) == 0
     return jax.shard_map(
-        body,
+        functools.partial(doubled_body, blk_size) if doubled else gathered_body,
         mesh=mesh,
         in_specs=placed,
         out_specs=(P(("groups", "blk")), P(("groups", "blk"))),

time: 93.8 us -> 36 us (0.38)
  blocking collectives: 78.4 us -> 0 us
  Pallas kernels: 0 us -> 12.8 us
  matrix products: 10.8 us -> 0 us
  waiting for transfers between devices: 0 us -> 9.19 us
  starting transfers between devices: 0 us -> 7.97 us
  local copies, waits for them, and re-layouts: 0.02 us -> 1.99 us
    all_gather x4 -> x0, blocking collectives: 78.4 us -> none  [the longest x1 23.8 us: body(): lax.all_gather(anchor, 'blk', axis=1, tiled=True)]
    pallas_call x0 -> x3, Pallas kernels: none -> 12.8 us  [the longest x1 4.84 us: doubled_body(): pl.pallas_call(functools.partial(own_kernel, assets), out_shape=(left_sha...]
    dot_general x3 -> x0, matrix products: 10.8 us -> none  [the longest x2 9.04 us: kernel_block(): lax.dot_general(source_states, sink_states, (((0,), (0,)), ((), ())), pre...]
    ppermute x0 -> x5, waiting for transfers between devices: none -> 9.19 us  [across(): return lax.ppermute(array, 'blk', [(i, i ^ mask) for i in range(blk_size)])]
    ppermute x0 -> x5, starting transfers between devices: none -> 7.97 us  [across(): return lax.ppermute(array, 'blk', [(i, i ^ mask) for i in range(blk_size)])]
    unnamed x4 -> x12, local copies, waits for them, and re-layouts: 0.01 us -> 1.98 us
    reduce_sum x2 -> x0, other arithmetic: 1.61 us -> none  [the longest x1 0.82 us: scaled_states(): anchor_half = 0.5 * jnp.sum(anchor * anchor, axis=0, keepdims=True)]
  transfers between devices with their start and end apart: 0 -> 5, of which waited for: 0 -> 4; matrix products, arithmetic and copies ran while one was open for 0% -> 0% of each run, Pallas kernels for 0% -> 14%
where the time goes in v1:
time: 36 us; the launch traced here: 35.5 us
  Pallas kernels  12.8 us (36%)
  waiting for transfers between devices  9.19 us (26%)
  starting transfers between devices  7.97 us (22%)
  between operations  2.02 us (6%)
  local copies, waits for them, and re-layouts  1.99 us (6%)
  other arithmetic  1.51 us (4%)
    ppermute x5, waiting for transfers between devices, across(): return lax.ppermute(array, 'blk', [(i, i ^ mask) for i in range(blk_size)])  9.19 us
    ppermute x5, starting transfers between devices, across(): return lax.ppermute(array, 'blk', [(i, i ^ mask) for i in range(blk_size)])  7.97 us
    pallas_call x1, Pallas kernels, doubled_body(): pl.pallas_call(functools.partial(own_kernel, assets), out_shape=(left_sha...  4.84 us
    pallas_call x1, Pallas kernels, doubled_body(): pl.pallas_call(functools.partial(other_kernel, assets), out_shape=(right_...  4.79 us
    pallas_call x1, Pallas kernels, doubled_body(): pl.pallas_call(functools.partial(weight_kernel, assets), grid=(1,), out_s...  3.22 us
    unnamed x12, local copies, waits for them, and re-layouts  1.98 us
    broadcast_in_dim x1, other arithmetic, doubled_body(): jnp.concatenate([current_states, next_states, next_values[None, :]], axis=0)  0.74 us
  transfers between devices with their start and end apart: 5, of which 4 were waited for; matrix products, arithmetic and copies ran while one was open for 0% of the time, Pallas kernels for 14%

profile of v1, /device:TPU:0, one launch (start us, length us, event | category | flops | bytes accessed | tf_op | source)
XLA Modules:
  0.0 35.5 jit_solution(2988081496787865210)
XLA Ops:
  0.6 0.0 copy-start.5
  0.6 0.7 %copy-done.5 = f32[256]{0:T(256)S(1)} copy-done((f32[256]{0:T(256)S(1)}, f32[256]{0:T(256)}, u32[]{:S(2)}) %copy-start.5) | copy-done | bytes 1048
  1.3 0.7 %maximum_bitcast_fusion = f32[1,33,256]{2,1,0:T(8,128)S(1)} fusion(f32[1,256]{1,0:T(1,128)S(1)} %bitcast.5, f32[16,256]{1,0:T(8,128)} %param.7, f32[16,256]{1,0:T(8,128)} %param.6), kind=kLoop, calls=%fused_computation.3 | loop fusion | flops 16896 | bytes 67584 | tf_op jit(solution)/shard_map/broadcast_in_dim | solution.py:256
  2.1 4.1 %collective-permute-start = (f32[1,33,256]{2,1,0:T(8,128)S(1)}, f32[1,33,256]{2,1,0:T(8,128)S(1)}, u32[]{:S(2)}, u32[]{:S(2)}) collective-permute-start(f32[1,33,256]{2,1,0:T(8,128)S(1)} %maximum_bitcast_fusion), channel_id=1, source_target_pairs={{0,8},{1,9},{2,10},{3,11},{4,12},{5,13},{6,14},{7,15},{8,0},{9,1},... | collective-permute-start | bytes 101384 | tf_op jit(solution)/shard_map/ppermute | solution.py:254
  6.1 2.4 %collective-permute-done = f32[1,33,256]{2,1,0:T(8,128)S(1)} collective-permute-done((f32[1,33,256]{2,1,0:T(8,128)S(1)}, f32[1,33,256]{2,1,0:T(8,128)S(1)}, u32[]{:S(2)}, u32[]{:S(2)}) %collective-permute-start) | collective-permute-done | bytes 33824 | tf_op jit(solution)/shard_map/ppermute | solution.py:254
  8.5 1.5 %collective-permute-start.1 = (f32[2,33,256]{2,1,0:T(8,128)S(1)}, f32[2,33,256]{2,1,0:T(8,128)S(1)}, u32[]{:S(2)}, u32[]{:S(2)}) collective-permute-start(f32[2,33,256]{2,1,0:T(8,128)S(1)} %pad_maximum_fusion.2), channel_id=1, source_target_pairs={{0,4},{1,5},{2,6},{3,7},{4,0},{5,1},{6,2},{7,3},{8,12},{9,13},{10,... | collective-permute-start | bytes 202760 | tf_op jit(solution)/shard_map/ppermute | solution.py:254
  10.1 3.0 %collective-permute-done.1 = f32[2,33,256]{2,1,0:T(8,128)S(1)} collective-permute-done((f32[2,33,256]{2,1,0:T(8,128)S(1)}, f32[2,33,256]{2,1,0:T(8,128)S(1)}, u32[]{:S(2)}, u32[]{:S(2)}) %collective-permute-start.1) | collective-permute-done | bytes 67616 | tf_op jit(solution)/shard_map/ppermute | solution.py:254
  13.1 1.8 %collective-permute-start.2 = (f32[4,33,256]{2,1,0:T(8,128)S(1)}, f32[4,33,256]{2,1,0:T(8,128)S(1)}, u32[]{:S(2)}, u32[]{:S(2)}) collective-permute-start(f32[4,33,256]{2,1,0:T(8,128)S(1)} %pad_maximum_fusion.1), channel_id=1, source_target_pairs={{0,2},{1,3},{2,0},{3,1},{4,6},{5,7},{6,4},{7,5},{8,10},{9,11},{10,... | collective-permute-start | bytes 405512 | tf_op jit(solution)/shard_map/ppermute | solution.py:254
  14.8 3.6 %collective-permute-done.2 = f32[4,33,256]{2,1,0:T(8,128)S(1)} collective-permute-done((f32[4,33,256]{2,1,0:T(8,128)S(1)}, f32[4,33,256]{2,1,0:T(8,128)S(1)}, u32[]{:S(2)}, u32[]{:S(2)}) %collective-permute-start.2) | collective-permute-done | bytes 135200 | tf_op jit(solution)/shard_map/ppermute | solution.py:254
  18.5 0.0 copy-start
  18.5 0.1 collective-permute-start.3
  19.3 0.0 copy-done
  19.3 4.8 %own_density.1 = (bf16[2048,128]{1,0:T(8,128)(2,1)}, bf16[128,2048]{1,0:T(8,128)(2,1)}, f32[1,2048]{1,0:T(1,128)}) custom-call(s32[1]{0:T(128)S(6)} %copy.8.index_ref, f32[12,16]{1,0:T(8,128)} %vol_ref.3, f32[8,33,256]{2,1,0:T(8,128)} %copy-done), custom_call_target="tpu_custom_call" | custom-call | flops 1073741824 | tf_op jit(solution)/shard_map/own_density/pallas_call | solution.py:269
  24.1 0.0 collective-permute-done.3.blocks_ref.others_ref
  24.1 0.0 copy-start.1
  24.1 0.7 %copy-done.1 = f32[8,17,256]{2,1,0:T(8,128)} copy-done((f32[8,17,256]{2,1,0:T(8,128)}, f32[8,17,256]{2,1,0:T(8,128)S(1)}, u32[]{:S(2)}) %copy-start.1) | copy-done | bytes 139288
  24.8 0.0 copy-start.4
  24.8 4.8 %other_density.1 = (bf16[128,2048]{1,0:T(8,128)(2,1)}, f32[1,2048]{1,0:T(1,128)}) custom-call(s32[1]{0:T(128)S(6)} %copy.8.index_ref, f32[12,16]{1,0:T(8,128)} %vol_ref.3, f32[8,17,256]{2,1,0:T(8,128)} %copy-done.1, bf16[2048,128]{1,0:T(8,128)(2,1)} %get-tuple-element.9.left_ref), custom_call_target="tpu_custom_call" | custom-call | flops 1073741824 | tf_op jit(solution)/shard_map/other_density/pallas_call | solution.py:277
  29.6 0.0 copy-done.4
  29.6 0.7 %pad_maximum_fusion.3.density_ref = f32[2,2048]{1,0:T(2,128)S(1)} fusion(f32[1,2048]{1,0:T(1,128)} %get-tuple-element.13, f32[1,2048]{1,0:T(1,128)S(1)} %copy-done.4), kind=kLoop, calls=%fused_computation.4 | loop fusion | flops 4096 | bytes 32768 | tf_op jit(solution)/shard_map/concatenate | solution.py:285
  30.3 0.0 copy-start.2
  30.3 0.5 %collective-permute-start.4 = (f32[2,2048]{1,0:T(2,128)S(1)}, f32[2,2048]{1,0:T(2,128)S(1)}, u32[]{:S(2)}, u32[]{:S(2)}) collective-permute-start(f32[2,2048]{1,0:T(2,128)S(1)} %pad_maximum_fusion.3.density_ref), channel_id=1, source_target_pairs={{0,1},{1,0},{2,3},{3,2},{4,5},{5,4},{6,7},{7,6},{8,9},{9,8},{10,11... | collective-permute-start | bytes 49160 | tf_op jit(solution)/shard_map/ppermute | solution.py:254
  31.5 0.2 collective-permute-done.4.received_ref
  31.7 0.0 copy-start.3
  31.7 0.0 copy-done.2
  31.7 0.6 %copy-done.3 = f32[2,2048]{1,0:T(2,128)} copy-done((f32[2,2048]{1,0:T(2,128)}, f32[2,2048]{1,0:T(2,128)S(1)}, u32[]{:S(2)}) %copy-start.3) | copy-done | bytes 16408
  32.3 3.2 %weights.1 = (f32[1,256]{1,0:T(1,128)}, f32[1,256]{1,0:T(1,128)}) custom-call(f32[1]{0:T(128)S(6)} %copy.9.strike_ref, f32[8,33,256]{2,1,0:T(8,128)} %copy-done, f32[8,17,256]{2,1,0:T(8,128)} %copy-done.1, bf16[2048,128]{1,0:T(8,128)(2,1)} %get-tuple-element.9.left_ref, bf16[128,2048]{1,0:T(8,128)(2,1)} %get-tuple-element.10.right_ref, ...), custom_call_target="tpu_custom_call" | custom-call | tf_op jit(solution)/shard_map/weights/pallas_call | solution.py:288
  (4 shorter events, 0.1 us)
Async XLA Ops:
  0.6 0.7 %copy-start.5 = (f32[256]{0:T(256)S(1)}, f32[256]{0:T(256)}, u32[]{:S(2)}) copy-start(f32[256]{0:T(256)} %param.8) | copy-start | bytes 3076
  2.1 6.5 %collective-permute-start = (f32[1,33,256]{2,1,0:T(8,128)S(1)}, f32[1,33,256]{2,1,0:T(8,128)S(1)}, u32[]{:S(2)}, u32[]{:S(2)}) collective-permute-start(f32[1,33,256]{2,1,0:T(8,128)S(1)} %maximum_bitcast_fusion), channel_id=1, source_target_pairs={{0,8},{1,9},{2,10},{3,11},{4,12},{5,13},{6,14},{7,15},{8,0},{9,1},... | collective-permute-start | bytes 101384 | tf_op jit(solution)/shard_map/ppermute | solution.py:254
  8.5 4.5 %collective-permute-start.1 = (f32[2,33,256]{2,1,0:T(8,128)S(1)}, f32[2,33,256]{2,1,0:T(8,128)S(1)}, u32[]{:S(2)}, u32[]{:S(2)}) collective-permute-start(f32[2,33,256]{2,1,0:T(8,128)S(1)} %pad_maximum_fusion.2), channel_id=1, source_target_pairs={{0,4},{1,5},{2,6},{3,7},{4,0},{5,1},{6,2},{7,3},{8,12},{9,13},{10,... | collective-permute-start | bytes 202760 | tf_op jit(solution)/shard_map/ppermute | solution.py:254
  13.1 5.4 %collective-permute-start.2 = (f32[4,33,256]{2,1,0:T(8,128)S(1)}, f32[4,33,256]{2,1,0:T(8,128)S(1)}, u32[]{:S(2)}, u32[]{:S(2)}) collective-permute-start(f32[4,33,256]{2,1,0:T(8,128)S(1)} %pad_maximum_fusion.1), channel_id=1, source_target_pairs={{0,2},{1,3},{2,0},{3,1},{4,6},{5,7},{6,4},{7,5},{8,10},{9,11},{10,... | collective-permute-start | bytes 405512 | tf_op jit(solution)/shard_map/ppermute | solution.py:254
  18.5 0.8 %copy-start = (f32[8,33,256]{2,1,0:T(8,128)}, f32[8,33,256]{2,1,0:T(8,128)S(1)}, u32[]{:S(2)}) copy-start(f32[8,33,256]{2,1,0:T(8,128)S(1)} %pad_maximum_fusion.blocks_ref) | copy-start | bytes 811012
  18.5 5.6 %collective-permute-start.3 = (f32[8,17,256]{2,1,0:T(8,128)S(1)}, f32[8,17,256]{2,1,0:T(8,128)S(1)}, u32[]{:S(2)}, u32[]{:S(2)}) collective-permute-start(f32[8,17,256]{2,1,0:T(8,128)S(1)} %slice.4), channel_id=1, source_target_pairs={{0,1},{1,0},{2,3},{3,2},{4,5},{5,4},{6,7},{7,6},{8,9},{9,8},{10,11... | collective-permute-start | bytes 417800 | tf_op jit(solution)/shard_map/ppermute | solution.py:254
  24.1 0.7 %copy-start.1 = (f32[8,17,256]{2,1,0:T(8,128)}, f32[8,17,256]{2,1,0:T(8,128)S(1)}, u32[]{:S(2)}) copy-start(f32[8,17,256]{2,1,0:T(8,128)S(1)} %collective-permute-done.3.blocks_ref.others_ref) | copy-start | bytes 417796
  24.8 4.8 %copy-start.4 = (f32[1,2048]{1,0:T(1,128)S(1)}, f32[1,2048]{1,0:T(1,128)}, u32[]{:S(2)}) copy-start(f32[1,2048]{1,0:T(1,128)} %get-tuple-element.12) | copy-start | bytes 24580
  30.3 1.4 %copy-start.2 = (f32[2,2048]{1,0:T(2,128)}, f32[2,2048]{1,0:T(2,128)S(1)}, u32[]{:S(2)}) copy-start(f32[2,2048]{1,0:T(2,128)S(1)} %pad_maximum_fusion.3.density_ref) | copy-start | bytes 49156
  30.3 1.4 %collective-permute-start.4 = (f32[2,2048]{1,0:T(2,128)S(1)}, f32[2,2048]{1,0:T(2,128)S(1)}, u32[]{:S(2)}, u32[]{:S(2)}) collective-permute-start(f32[2,2048]{1,0:T(2,128)S(1)} %pad_maximum_fusion.3.density_ref), channel_id=1, source_target_pairs={{0,1},{1,0},{2,3},{3,2},{4,5},{5,4},{6,7},{7,6},{8,9},{9,8},{10,11... | collective-permute-start | bytes 49160 | tf_op jit(solution)/shard_map/ppermute | solution.py:254
  31.7 0.6 %copy-start.3 = (f32[2,2048]{1,0:T(2,128)}, f32[2,2048]{1,0:T(2,128)S(1)}, u32[]{:S(2)}) copy-start(f32[2,2048]{1,0:T(2,128)S(1)} %collective-permute-done.4.received_ref) | copy-start | bytes 49156

commit v2 on v0

--- a/solution.py
+++ b/solution.py
@@ -1,12 +1,21 @@
+import functools
 import math
 
 import jax
 import jax.numpy as jnp
 from jax import lax
+from jax.experimental import pallas as pl
+from jax.experimental.pallas import tpu as pltpu
 from jax.sharding import PartitionSpec as P
 
 rate_year = 0.05
 step_years = 0.1
+log2_e = math.log2(math.e)
+lanes = 128
+lane_tile = 512
+row_tile = 256
+depth = 128
+vmem_grant = 16 * 1024 * 1024
 
 
 def scaled_states(current_states, next_states, vol_table, date_index):
@@ -45,7 +54,7 @@
     return (continuation, jnp.maximum(payoff, continuation))
 
 
-def body(current_states, next_states, next_values, vol_table, date_index, strike):
+def gathered_body(current_states, next_states, next_values, vol_table, date_index, strike):
     anchor, anchor_half, target, target_half = scaled_states(
         current_states, next_states, vol_table, date_index
     )
@@ -57,7 +66,7 @@
     row_count = pieces[0].shape[1]
     block_size = block_rows(row_count)
 
-    def one_block(number, inner_sum):
+    def density_block(number, inner_sum):
         source_part = lax.dynamic_slice_in_dim(pieces[0], number * block_size, block_size, 1)
         norm_part = lax.dynamic_slice_in_dim(pieces[1], number * block_size, block_size, 1)
         return inner_sum + jnp.sum(
@@ -65,7 +74,7 @@
         )
 
     density = lax.fori_loop(
-        0, row_count // block_size, one_block, jnp.zeros((local_count,), jnp.float32)
+        0, row_count // block_size, density_block, jnp.zeros((local_count,), jnp.float32)
     )
     extras = jnp.concatenate(
         [target_half, (next_values / density)[None, :], (1.0 / density)[None, :]], axis=0
@@ -74,16 +83,10 @@
         lax.all_gather(target, "blk", axis=1, tiled=True),
         lax.all_gather(extras, "blk", axis=1, tiled=True),
     )
-    row_count = add_pieces[0].shape[1]
-    add_block_size = block_rows(row_count)
-
-    def one_block(number, inner_sum):
-        sink_part = lax.dynamic_slice_in_dim(
-            add_pieces[0], number * add_block_size, add_block_size, 1
-        )
-        extra_part = lax.dynamic_slice_in_dim(
-            add_pieces[1], number * add_block_size, add_block_size, 1
-        )
+
+    def weighted_block(number, inner_sum):
+        sink_part = lax.dynamic_slice_in_dim(add_pieces[0], number * block_size, block_size, 1)
+        extra_part = lax.dynamic_slice_in_dim(add_pieces[1], number * block_size, block_size, 1)
         weights = kernel_block(sink_part, extra_part[0:1], anchor, anchor_half)
         return inner_sum + jnp.dot(
             extra_part[1:3],
@@ -93,12 +96,350 @@
         )
 
     totals = lax.fori_loop(
-        0, row_count // add_block_size, one_block, jnp.zeros((2, local_count), jnp.float32)
+        0, row_count // block_size, weighted_block, jnp.zeros((2, local_count), jnp.float32)
     )
     return finish(current_states, totals, strike)
 
 
+def in_three(x):
+    first = x.astype(jnp.bfloat16)
+    rest = x - first.astype(jnp.float32)
+    second = rest.astype(jnp.bfloat16)
+    third = (rest - second.astype(jnp.float32)).astype(jnp.bfloat16)
+    return first, second, third
+
+
+def with_norm(pieces, norm, shift):
+    rows = lax.broadcasted_iota(jnp.int32, (16, norm.shape[1]), 0)
+    tile = jnp.where((rows >= 3 - shift) & (rows < 6 - shift), 1.0, 0.0)
+    for k, part in enumerate(in_three(norm)):
+        tile = jnp.where(rows == k + shift, part.astype(jnp.float32), tile)
+    stacked = list(pieces) + [tile.astype(jnp.bfloat16)]
+    height = sum(piece.shape[0] for piece in stacked)
+    stacked.append(jnp.zeros((depth - height, norm.shape[1]), jnp.bfloat16))
+    return jnp.concatenate(stacked, axis=0)
+
+
+def source_operand(states, inverse, drift_term):
+    anchor = (states + drift_term) * inverse
+    half = (0.5 * log2_e) * jnp.sum(anchor * anchor, axis=0, keepdims=True)
+    a1, a2, a3 = in_three(anchor * log2_e)
+    return with_norm((a1, a1, a2, a1, a2, a3), -half, 0).T
+
+
+def sink_operand(states, inverse):
+    target = states * inverse
+    half = (0.5 * log2_e) * jnp.sum(target * target, axis=0, keepdims=True)
+    t1, t2, t3 = in_three(target)
+    return with_norm((t1, t2, t1, t3, t2, t1), -half, 3)
+
+
+def build_sources(states_ref, columns_ref, left_ref):
+    inverse, drift_term = columns_ref[0], columns_ref[1]
+    assets = inverse.shape[0]
+    for slab in range(left_ref.shape[0] // lanes):
+        states = states_ref[slab * assets : (slab + 1) * assets, :]
+        left_ref[slab * lanes : (slab + 1) * lanes, :] = source_operand(states, inverse, drift_term)
+
+
+def build_sinks(states_ref, start, columns_ref, right_ref):
+    inverse = columns_ref[0]
+    assets = inverse.shape[0]
+    for slab in range(right_ref.shape[1] // lanes):
+        states = states_ref[start + slab * assets : start + (slab + 1) * assets, :]
+        right_ref[:, slab * lanes : (slab + 1) * lanes] = sink_operand(states, inverse)
+
+
+def add_density(left_refs, right_ref, density_ref, first_row, base_ref):
+    width = math.gcd(right_ref.shape[1], lane_tile)
+    for number in range(right_ref.shape[1] // width):
+        right = right_ref[:, number * width : (number + 1) * width]
+        total = jnp.zeros((8, width), jnp.float32)
+        for left_ref in left_refs:
+            height = math.gcd(left_ref.shape[0], row_tile)
+            for k in range(left_ref.shape[0] // height):
+                exponent = jnp.dot(
+                    left_ref[k * height : (k + 1) * height, :],
+                    right,
+                    preferred_element_type=jnp.float32,
+                )
+                total += jnp.sum(jnp.exp2(exponent).reshape(height // 8, 8, width), axis=0)
+        sums = jnp.sum(total, axis=0, keepdims=True)
+        for slab in range(width // lanes):
+            row = number * (width // lanes) + slab
+            value = sums[:, slab * lanes : (slab + 1) * lanes]
+            if base_ref is not None:
+                value += base_ref[row : row + 1, :]
+            density_ref[first_row + row : first_row + row + 1, :] = value
+
+
+def pack_kernel(*refs):
+    row = 0
+    for ref in refs[:-1]:
+        height = min(ref.shape[0], refs[-1].shape[0] - row)
+        refs[-1][row : row + height, :] = ref[0:height, :]
+        row += height
+
+
+def side_kernel(table_ref, packed_ref, columns_ref, payoff_ref):
+    dates, assets = table_ref.shape[0] - 1, table_ref.shape[1]
+    index = table_ref[dates : dates + 1, 0:1]
+    strike = table_ref[dates : dates + 1, 1:2]
+    rows = lax.broadcasted_iota(jnp.int32, (dates, assets), 0).astype(jnp.float32)
+    vol_row = jnp.sum(
+        jnp.where(rows == index, table_ref[0:dates, :], 0.0), axis=0, keepdims=True
+    )
+    square = (assets, assets)
+    diagonal = lax.broadcasted_iota(jnp.int32, square, 0) == lax.broadcasted_iota(
+        jnp.int32, square, 1
+    )
+    vol = jnp.sum(
+        jnp.where(diagonal, jnp.broadcast_to(vol_row, square), 0.0), axis=1, keepdims=True
+    )
+    vol = jnp.broadcast_to(vol, (assets, lanes))
+    columns_ref[0] = 1.0 / (vol * math.sqrt(step_years))
+    columns_ref[1] = (rate_year - 0.5 * vol * vol) * step_years
+    for slab in range(payoff_ref.shape[0]):
+        prices = jnp.exp(packed_ref[slab * assets : (slab + 1) * assets, :])
+        best = jnp.max(prices, axis=0, keepdims=True)
+        payoff_ref[slab : slab + 1, :] = jnp.maximum(best - strike, 0.0)
+
+
+def column_kernel(sources, columns_ref, packed_ref, left_ref, right_ref, density_ref):
+    build_sources(packed_ref, columns_ref, left_ref)
+    build_sinks(packed_ref, sources, columns_ref, right_ref)
+    add_density((left_ref,), right_ref, density_ref, 0, None)
+
+
+def column_other_kernel(columns_ref, other_ref, left_ref, right_ref, density_ref):
+    build_sinks(other_ref, 0, columns_ref, right_ref)
+    add_density((left_ref,), right_ref, density_ref, 0, None)
+
+
+def far_kernel(
+    sources,
+    columns_ref,
+    packed_ref,
+    left_ref,
+    right_ref,
+    base_ref,
+    far_left_ref,
+    far_right_ref,
+    density_ref,
+):
+    build_sources(packed_ref, columns_ref, far_left_ref)
+    build_sinks(packed_ref, sources, columns_ref, far_right_ref)
+    add_density((far_left_ref,), right_ref, density_ref, 0, base_ref)
+    add_density((left_ref, far_left_ref), far_right_ref, density_ref, base_ref.shape[0], None)
+
+
+def far_other_kernel(
+    columns_ref,
+    other_ref,
+    left_ref,
+    far_left_ref,
+    right_ref,
+    base_ref,
+    far_right_ref,
+    density_ref,
+):
+    build_sinks(other_ref, 0, columns_ref, far_right_ref)
+    add_density((far_left_ref,), right_ref, density_ref, 0, base_ref)
+    add_density((left_ref, far_left_ref), far_right_ref, density_ref, base_ref.shape[0], None)
+
+
+def matrix_kernel(left_ref, *refs):
+    matrix_ref = refs[-1]
+    place = 0
+    for right_ref in refs[:-1]:
+        width = math.gcd(right_ref.shape[1], lane_tile)
+        for number in range(right_ref.shape[1] // width):
+            matrix_ref[:, place : place + width] = jnp.exp2(
+                jnp.dot(
+                    left_ref[...],
+                    right_ref[:, number * width : (number + 1) * width],
+                    preferred_element_type=jnp.float32,
+                )
+            )
+            place += width
+
+
+def weight_kernel(
+    values_start,
+    matrix_ref,
+    density_ref,
+    received_ref,
+    packed_ref,
+    far_packed_ref,
+    other_ref,
+    far_other_ref,
+    payoff_ref,
+    continuation_ref,
+    node_ref,
+    ratio_ref,
+):
+    slabs = density_ref.shape[0]
+    half = slabs // 2
+    quarter = half // 2
+    inverse = 1.0 / jnp.concatenate(
+        [
+            density_ref[:half, :] + received_ref[half:, :],
+            density_ref[half:, :] + received_ref[:half, :],
+        ],
+        axis=0,
+    )
+    ratio_ref[1] = inverse
+    other_start = other_ref.shape[0] - quarter
+    for k, (values_ref, start) in enumerate(
+        (
+            (packed_ref, values_start),
+            (far_packed_ref, values_start),
+            (other_ref, other_start),
+            (far_other_ref, other_start),
+        )
+    ):
+        part = slice(k * quarter, (k + 1) * quarter)
+        ratio_ref[0, part, :] = values_ref[start : start + quarter, :] * inverse[part]
+    count = matrix_ref.shape[0]
+    height = math.gcd(count, 64)
+    sums = []
+    for k in range(count // height):
+        weighted = jnp.zeros((height, lanes), jnp.float32)
+        mass = jnp.zeros((height, lanes), jnp.float32)
+        for slab in range(slabs):
+            piece = matrix_ref[k * height : (k + 1) * height, slab * lanes : (slab + 1) * lanes]
+            weighted += piece * ratio_ref[0, slab : slab + 1, :]
+            mass += piece * ratio_ref[1, slab : slab + 1, :]
+        sums.append((weighted, mass))
+    per_slab = lanes // height
+    for slab in range(count // lanes):
+        group = sums[slab * per_slab : (slab + 1) * per_slab]
+        weighted, mass = (
+            jnp.sum(jnp.concatenate([pair[k] for pair in group], axis=0).T, axis=0, keepdims=True)
+            for k in range(2)
+        )
+        continuation = math.exp(-rate_year * step_years) * weighted / mass
+        continuation_ref[slab : slab + 1, :] = continuation
+        node_ref[slab : slab + 1, :] = jnp.maximum(payoff_ref[slab : slab + 1, :], continuation)
+
+
+vmem = pl.BlockSpec(memory_space=pltpu.VMEM)
+
+
+def local_call(kernel, name, in_specs, out_shapes, matmul_pairs=0, scratch_shapes=()):
+    cost = pl.CostEstimate(
+        flops=2 * depth * matmul_pairs, transcendentals=matmul_pairs, bytes_accessed=0
+    )
+    return pl.pallas_call(
+        kernel,
+        out_shape=out_shapes,
+        in_specs=in_specs,
+        out_specs=[vmem] * len(out_shapes),
+        scratch_shapes=scratch_shapes,
+        cost_estimate=cost,
+        compiler_params=pltpu.CompilerParams(vmem_limit_bytes=vmem_grant),
+        name=name,
+    )
+
+
+def doubled_body(blk_size, current_states, next_states, next_values, vol_table, date_index, strike):
+    assets, count = current_states.shape
+    own_slabs = count // lanes
+
+    def across(array, mask):
+        return lax.ppermute(array, "blk", [(i, i ^ mask) for i in range(blk_size)])
+
+    def floats(*shape):
+        return jax.ShapeDtypeStruct(shape, jnp.float32)
+
+    def halves(*shape):
+        return jax.ShapeDtypeStruct(shape, jnp.bfloat16)
+
+    pieces = [
+        part[:, slab * lanes : (slab + 1) * lanes]
+        for part in (current_states, next_states)
+        for slab in range(own_slabs)
+    ]
+    rows = lax.pad(
+        next_values.reshape(own_slabs, lanes), jnp.float32(0), ((0, assets - own_slabs, 0), (0, 0, 0))
+    )
+    tile_rows = lax.broadcasted_iota(jnp.int32, rows.shape, 0)
+    pieces.append(jnp.where(tile_rows < own_slabs, rows, pieces[0]))
+    (packed,) = local_call(
+        pack_kernel,
+        "pack",
+        [vmem] * len(pieces),
+        [floats((2 * assets + 1) * own_slabs, lanes)],
+    )(*pieces)
+    places = lax.broadcasted_iota(jnp.int32, (1, assets), 1)
+    last = jnp.where(places == 0, date_index.astype(jnp.float32), jnp.where(places == 1, strike, 0.0))
+    table = jnp.concatenate([vol_table, last], axis=0)
+    columns, payoff = local_call(
+        side_kernel, "side", [vmem, vmem], [floats(2, assets, lanes), floats(own_slabs, lanes)]
+    )(table, packed)
+
+    slabs = own_slabs
+    mask = blk_size // 2
+    while mask > 2:
+        received = across(packed, mask)
+        cuts = (0, assets * slabs, 2 * assets * slabs, (2 * assets + 1) * slabs)
+        packed = jnp.concatenate(
+            [part[a:b] for a, b in zip(cuts, cuts[1:]) for part in (packed, received)], axis=0
+        )
+        if slabs == own_slabs:
+            packed, columns, payoff = lax.optimization_barrier((packed, columns, payoff))
+        slabs *= 2
+        mask //= 2
+    sources = assets * slabs
+    nodes = slabs * lanes
+    far = across(packed, 2)
+    other = across(packed[sources:], 1)
+    left, right, base = local_call(
+        functools.partial(column_kernel, sources),
+        "column",
+        [vmem, vmem],
+        [halves(nodes, depth), halves(depth, nodes), floats(slabs, lanes)],
+        nodes * nodes,
+    )(columns, packed)
+    other_right, other_base = local_call(
+        column_other_kernel,
+        "column_other",
+        [vmem] * 3,
+        [halves(depth, nodes), floats(slabs, lanes)],
+        nodes * nodes,
+    )(columns, other, left)
+    far_other = across(far[sources:], 1)
+    far_left, far_right, density = local_call(
+        functools.partial(far_kernel, sources),
+        "far",
+        [vmem] * 5,
+        [halves(nodes, depth), halves(depth, nodes), floats(2 * slabs, lanes)],
+        3 * nodes * nodes,
+    )(columns, far, left, right, base)
+    far_other_right, other_density = local_call(
+        far_other_kernel,
+        "far_other",
+        [vmem] * 6,
+        [halves(depth, nodes), floats(2 * slabs, lanes)],
+        3 * nodes * nodes,
+    )(columns, far_other, left, far_left, other_right, other_base)
+    density = jnp.concatenate([density, other_density], axis=0)
+    received = across(density, 1)
+    (matrix,) = local_call(
+        matrix_kernel, "matrix", [vmem] * 5, [floats(count, 4 * nodes)], 4 * count * nodes
+    )(left[:count], right, far_right, other_right, far_other_right)
+    continuation, node_value = local_call(
+        functools.partial(weight_kernel, 2 * sources),
+        "weights",
+        [vmem] * 8,
+        [floats(own_slabs, lanes)] * 2,
+        scratch_shapes=[pltpu.VMEM((2, 4 * slabs, lanes), jnp.float32)],
+    )(matrix, density, received, packed, far, other, far_other, payoff)
+    return continuation.reshape(count), node_value.reshape(count)
+
+
 def solution(mesh):
+    blk_size = mesh.shape["blk"]
     placed = (
         P(None, ("groups", "blk")),
         P(None, ("groups", "blk")),
@@ -107,8 +448,9 @@
         P(),
         P(),
     )
+    doubled = blk_size in (16, 32)
     return jax.shard_map(
-        body,
+        functools.partial(doubled_body, blk_size) if doubled else gathered_body,
         mesh=mesh,
         in_specs=placed,
         out_specs=(P(("groups", "blk")), P(("groups", "blk"))),

time: 93.8 us -> 24.2 us (0.26)
  blocking collectives: 78.4 us -> 0 us
  matrix products: 10.8 us -> 0 us
  starting transfers between devices: 0 us -> 8.07 us
  Pallas kernels: 0 us -> 7.39 us
  waiting for transfers between devices: 0 us -> 4.78 us
    all_gather x4 -> x0, blocking collectives: 78.4 us -> none  [the longest x1 23.8 us: body(): lax.all_gather(anchor, 'blk', axis=1, tiled=True)]
    dot_general x3 -> x0, matrix products: 10.8 us -> none  [the longest x2 9.04 us: kernel_block(): lax.dot_general(source_states, sink_states, (((0,), (0,)), ((), ())), pre...]
    ppermute x0 -> x6, starting transfers between devices: none -> 8.07 us  [across(): return lax.ppermute(array, 'blk', [(i, i ^ mask) for i in range(blk_size)])]
    pallas_call x0 -> x8, Pallas kernels: none -> 7.39 us  [the longest x1 1.87 us: doubled_body(): local_call(functools.partial(far_kernel, sources), 'far', [vmem] * 5, [ha...]
    ppermute x0 -> x6, waiting for transfers between devices: none -> 4.78 us  [across(): return lax.ppermute(array, 'blk', [(i, i ^ mask) for i in range(blk_size)])]
    reduce_sum x2 -> x0, other arithmetic: 1.61 us -> none  [the longest x1 0.82 us: scaled_states(): anchor_half = 0.5 * jnp.sum(anchor * anchor, axis=0, keepdims=True)]
  transfers between devices with their start and end apart: 0 -> 6, of which waited for: 0 -> 5; matrix products, arithmetic and copies ran while one was open for 0% -> 3% of each run, Pallas kernels for 0% -> 18%
where the time goes in v2:
time: 24.2 us; the launch traced here: 24 us
  starting transfers between devices  8.07 us (33%)
  Pallas kernels  7.39 us (31%)
  waiting for transfers between devices  4.78 us (20%)
  between operations  2.05 us (8%)
  other arithmetic  1.57 us (6%)
    ppermute x6, starting transfers between devices, across(): return lax.ppermute(array, 'blk', [(i, i ^ mask) for i in range(blk_size)])  8.07 us
    ppermute x6, waiting for transfers between devices, across(): return lax.ppermute(array, 'blk', [(i, i ^ mask) for i in range(blk_size)])  4.78 us
    pallas_call x1, Pallas kernels, doubled_body(): local_call(functools.partial(far_kernel, sources), 'far', [vmem] * 5, [ha...  1.87 us
    pallas_call x1, Pallas kernels, doubled_body(): local_call(far_other_kernel, 'far_other', [vmem] * 6, [halves(depth, node...  1.79 us
    pallas_call x1, Pallas kernels, doubled_body(): local_call(functools.partial(weight_kernel, 2 * sources), 'weights', [vme...  1.38 us
    select_n x1, other arithmetic, doubled_body(): pieces.append(jnp.where(tile_rows < own_slabs, rows, pieces[0]))  0.84 us
    pallas_call x1, Pallas kernels, doubled_body(): local_call(functools.partial(column_kernel, sources), 'column', [vmem, vm...  0.79 us
    pallas_call x1, Pallas kernels, doubled_body(): local_call(column_other_kernel, 'column_other', [vmem] * 3, [halves(depth...  0.74 us
  transfers between devices with their start and end apart: 6, of which 5 were waited for; matrix products, arithmetic and copies ran while one was open for 3% of the time, Pallas kernels for 18%

profile of v2, /device:TPU:0, one launch (start us, length us, event | category | flops | bytes accessed | tf_op | source)
XLA Modules:
  0.0 24.0 jit_solution(7493879311219478878)
XLA Ops:
  0.6 0.8 %pad_select_fusion = (f32[16,128]{1,0:T(8,128)S(1)}, f32[16,128]{1,0:T(8,128)S(1)}, f32[16,128]{1,0:T(8,128)S(1)}, f32[16,128]{1,0:T(8,128)S(1)}, f32[16,128]{1,0:T(8,128)S(1)}) fusion(f32[2,128]{1,0:T(2,128)} %bitcast.6, pred[16]{0:T(512)(128)(4,1)S(1)} %iota_compare_fusion, f32[16,256]{1,0:T(8,128)} %param.6, f32[16,256]{1,0:T(8,128)} %param.7), kind=kLoop, calls=%fused_computation.2 | loop fusion | flops 2048 | bytes 74768 | tf_op jit(solution)/shard_map/jit(_where)/select_n | solution.py:367
  1.5 4.1 %collective-permute-start = (f32[66,128]{1,0:T(8,128)S(1)}, f32[66,128]{1,0:T(8,128)S(1)}, u32[]{:S(2)}, u32[]{:S(2)}) collective-permute-start(f32[66,128]{1,0:T(8,128)S(1)} %pack.1.packed_ref), channel_id=1, source_target_pairs={{0,8},{1,9},{2,10},{3,11},{4,12},{5,13},{6,14},{7,15},{8,0},{9,1},... | collective-permute-start | bytes 101384 | tf_op jit(solution)/shard_map/ppermute | solution.py:350
  6.9 0.7 %pad_maximum_fusion.1.table_ref = f32[13,16]{1,0:T(8,128)S(1)} fusion(f32[1,16]{1,0:T(1,128)S(1)} %compare_select_fusion.1, f32[12,16]{1,0:T(8,128)} %param.9), kind=kLoop, calls=%fused_computation.1 | loop fusion | flops 208 | bytes 1664 | tf_op jit(solution)/shard_map/concatenate | solution.py:376
  7.6 0.1 side.1
  7.8 0.2 collective-permute-done
  8.0 1.6 %collective-permute-start.1 = (f32[132,128]{1,0:T(8,128)S(1)}, f32[132,128]{1,0:T(8,128)S(1)}, u32[]{:S(2)}, u32[]{:S(2)}) collective-permute-start(f32[132,128]{1,0:T(8,128)S(1)} %concatenate.15), channel_id=1, source_target_pairs={{0,4},{1,5},{2,6},{3,7},{4,0},{5,1},{6,2},{7,3},{8,12},{9,13},{10,... | collective-permute-start | bytes 202760 | tf_op jit(solution)/shard_map/ppermute | solution.py:350
  9.6 2.8 %collective-permute-done.1 = f32[132,128]{1,0:T(8,128)S(1)} collective-permute-done((f32[132,128]{1,0:T(8,128)S(1)}, f32[132,128]{1,0:T(8,128)S(1)}, u32[]{:S(2)}, u32[]{:S(2)}) %collective-permute-start.1) | collective-permute-done | bytes 67616 | tf_op jit(solution)/shard_map/ppermute | solution.py:350
  12.4 1.8 %collective-permute-start.2 = (f32[264,128]{1,0:T(8,128)S(1)}, f32[264,128]{1,0:T(8,128)S(1)}, u32[]{:S(2)}, u32[]{:S(2)}) collective-permute-start(f32[264,128]{1,0:T(8,128)S(1)} %concatenate.17.packed_ref), channel_id=1, source_target_pairs={{0,2},{1,3},{2,0},{3,1},{4,6},{5,7},{6,4},{7,5},{8,10},{9,11},{10,... | collective-permute-start | bytes 405512 | tf_op jit(solution)/shard_map/ppermute | solution.py:350
  14.2 0.1 collective-permute-start.3
  14.2 0.8 %column.1 = (bf16[1024,128]{1,0:T(8,128)(2,1)S(1)}, bf16[128,1024]{1,0:T(8,128)(2,1)S(1)}, f32[8,128]{1,0:T(8,128)S(1)}) custom-call(f32[2,16,128]{2,1,0:T(8,128)S(1)} %get-tuple-element.21.columns_ref, f32[264,128]{1,0:T(8,128)S(1)} %concatenate.17.packed_ref), custom_call_target="tpu_custom_call" | custom-call | flops 268435456 | tf_op jit(solution)/shard_map/column/pallas_call | solution.py:397
  15.0 0.4 %collective-permute-done.3.other_ref = f32[136,128]{1,0:T(8,128)S(1)} collective-permute-done((f32[136,128]{1,0:T(8,128)S(1)}, f32[136,128]{1,0:T(8,128)S(1)}, u32[]{:S(2)}, u32[]{:S(2)}) %collective-permute-start.3) | collective-permute-done | bytes 69664 | tf_op jit(solution)/shard_map/ppermute | solution.py:350
  15.5 0.7 %column_other.1 = (bf16[128,1024]{1,0:T(8,128)(2,1)S(1)}, f32[8,128]{1,0:T(8,128)S(1)}) custom-call(f32[2,16,128]{2,1,0:T(8,128)S(1)} %get-tuple-element.21.columns_ref, f32[136,128]{1,0:T(8,128)S(1)} %collective-permute-done.3.other_ref, bf16[1024,128]{1,0:T(8,128)(2,1)S(1)} %get-tuple-element.23.left_ref), custom_call_target="tpu_custom_call" | custom-call | flops 268435456 | tf_op jit(solution)/shard_map/column_other/pallas_call | solution.py:404
  16.2 1.2 %collective-permute-done.2.packed_ref.far_packed_ref = f32[264,128]{1,0:T(8,128)S(1)} collective-permute-done((f32[264,128]{1,0:T(8,128)S(1)}, f32[264,128]{1,0:T(8,128)S(1)}, u32[]{:S(2)}, u32[]{:S(2)}) %collective-permute-start.2) | collective-permute-done | bytes 135200 | tf_op jit(solution)/shard_map/ppermute | solution.py:350
  17.5 0.0 collective-permute-start.4
  17.5 1.9 %far.1 = (bf16[1024,128]{1,0:T(8,128)(2,1)S(1)}, bf16[128,1024]{1,0:T(8,128)(2,1)S(1)}, f32[16,128]{1,0:T(8,128)S(1)}) custom-call(f32[2,16,128]{2,1,0:T(8,128)S(1)} %get-tuple-element.21.columns_ref, f32[264,128]{1,0:T(8,128)S(1)} %collective-permute-done.2.packed_ref.far_packed_ref, bf16[1024,128]{1,0:T(8,128)(2,1)S(1)} %get-tuple-element.23.left_ref, ...), custom_call_target="tpu_custom_call" | custom-call | flops 805306368 | tf_op jit(solution)/shard_map/far/pallas_call | solution.py:412
  19.4 0.0 collective-permute-done.4.other_ref.far_other_ref
  19.4 1.8 %far_other.1 = (bf16[128,1024]{1,0:T(8,128)(2,1)S(1)}, f32[16,128]{1,0:T(8,128)S(1)}) custom-call(f32[2,16,128]{2,1,0:T(8,128)S(1)} %get-tuple-element.21.columns_ref, f32[136,128]{1,0:T(8,128)S(1)} %collective-permute-done.4.other_ref.far_other_ref, bf16[1024,128]{1,0:T(8,128)(2,1)S(1)} %get-tuple-element.23.left_ref, ...), custom_call_target="tpu_custom_call" | custom-call | flops 805306368 | tf_op jit(solution)/shard_map/far_other/pallas_call | solution.py:419
  21.2 0.6 %collective-permute-start.5 = (f32[32,128]{1,0:T(8,128)S(1)}, f32[32,128]{1,0:T(8,128)S(1)}, u32[]{:S(2)}, u32[]{:S(2)}) collective-permute-start(f32[32,128]{1,0:T(8,128)S(1)} %constant_dynamic-update-slice_fusion.density_ref), channel_id=1, source_target_pairs={{0,1},{1,0},{2,3},{3,2},{4,5},{5,4},{6,7},{7,6},{8,9},{9,8},{10,11... | collective-permute-start | bytes 49160 | tf_op jit(solution)/shard_map/ppermute | solution.py:350
  21.7 0.7 %matrix.1.matrix_ref = f32[256,4096]{1,0:T(8,128)S(1)} custom-call(bf16[256,128]{1,0:T(8,128)(2,1)S(1)} %slice.72.left_ref, bf16[128,1024]{1,0:T(8,128)(2,1)S(1)} %get-tuple-element.24.right_ref.refs_0_, bf16[128,1024]{1,0:T(8,128)(2,1)S(1)} %get-tuple-element.26.refs_1_, bf16[128,1024]{1,0:T(8,128)(2,1)S(1)} %get-tuple-element.27.right_ref.refs_2_, ...), custom_call_target="tpu_custom_call" | custom-call | flops 268435456 | tf_op jit(solution)/shard_map/matrix/pallas_call | solution.py:428
  22.4 0.1 collective-permute-done.5.received_ref
  22.6 1.4 %weights.1 = (f32[2,128]{1,0:T(2,128)}, f32[2,128]{1,0:T(2,128)}) custom-call(f32[256,4096]{1,0:T(8,128)S(1)} %matrix.1.matrix_ref, f32[32,128]{1,0:T(8,128)S(1)} %constant_dynamic-update-slice_fusion.density_ref, f32[32,128]{1,0:T(8,128)S(1)} %collective-permute-done.5.received_ref, f32[264,128]{1,0:T(8,128)S(1)} %concatenate.17.packed_ref, ...), custom_call_target="tpu_custom_call" | custom-call | tf_op jit(solution)/shard_map/weights/pallas_call | solution.py:431
  (18 shorter events, 0.1 us)
Async XLA Ops:
  1.5 6.5 %collective-permute-start = (f32[66,128]{1,0:T(8,128)S(1)}, f32[66,128]{1,0:T(8,128)S(1)}, u32[]{:S(2)}, u32[]{:S(2)}) collective-permute-start(f32[66,128]{1,0:T(8,128)S(1)} %pack.1.packed_ref), channel_id=1, source_target_pairs={{0,8},{1,9},{2,10},{3,11},{4,12},{5,13},{6,14},{7,15},{8,0},{9,1},... | collective-permute-start | bytes 101384 | tf_op jit(solution)/shard_map/ppermute | solution.py:350
  8.0 4.4 %collective-permute-start.1 = (f32[132,128]{1,0:T(8,128)S(1)}, f32[132,128]{1,0:T(8,128)S(1)}, u32[]{:S(2)}, u32[]{:S(2)}) collective-permute-start(f32[132,128]{1,0:T(8,128)S(1)} %concatenate.15), channel_id=1, source_target_pairs={{0,4},{1,5},{2,6},{3,7},{4,0},{5,1},{6,2},{7,3},{8,12},{9,13},{10,... | collective-permute-start | bytes 202760 | tf_op jit(solution)/shard_map/ppermute | solution.py:350
  12.4 5.1 %collective-permute-start.2 = (f32[264,128]{1,0:T(8,128)S(1)}, f32[264,128]{1,0:T(8,128)S(1)}, u32[]{:S(2)}, u32[]{:S(2)}) collective-permute-start(f32[264,128]{1,0:T(8,128)S(1)} %concatenate.17.packed_ref), channel_id=1, source_target_pairs={{0,2},{1,3},{2,0},{3,1},{4,6},{5,7},{6,4},{7,5},{8,10},{9,11},{10,... | collective-permute-start | bytes 405512 | tf_op jit(solution)/shard_map/ppermute | solution.py:350
  14.2 1.3 %collective-permute-start.3 = (f32[136,128]{1,0:T(8,128)S(1)}, f32[136,128]{1,0:T(8,128)S(1)}, u32[]{:S(2)}, u32[]{:S(2)}) collective-permute-start(f32[136,128]{1,0:T(8,128)S(1)} %pad_maximum_fusion), channel_id=1, source_target_pairs={{0,1},{1,0},{2,3},{3,2},{4,5},{5,4},{6,7},{7,6},{8,9},{9,8},{10,11... | collective-permute-start | bytes 208904 | tf_op jit(solution)/shard_map/ppermute | solution.py:350
  17.5 1.9 %collective-permute-start.4 = (f32[136,128]{1,0:T(8,128)S(1)}, f32[136,128]{1,0:T(8,128)S(1)}, u32[]{:S(2)}, u32[]{:S(2)}) collective-permute-start(f32[136,128]{1,0:T(8,128)S(1)} %slice.83), channel_id=1, source_target_pairs={{0,1},{1,0},{2,3},{3,2},{4,5},{5,4},{6,7},{7,6},{8,9},{9,8},{10,11... | collective-permute-start | bytes 208904 | tf_op jit(solution)/shard_map/ppermute | solution.py:350
  21.2 1.4 %collective-permute-start.5 = (f32[32,128]{1,0:T(8,128)S(1)}, f32[32,128]{1,0:T(8,128)S(1)}, u32[]{:S(2)}, u32[]{:S(2)}) collective-permute-start(f32[32,128]{1,0:T(8,128)S(1)} %constant_dynamic-update-slice_fusion.density_ref), channel_id=1, source_target_pairs={{0,1},{1,0},{2,3},{3,2},{4,5},{5,4},{6,7},{7,6},{8,9},{9,8},{10,11... | collective-permute-start | bytes 49160 | tf_op jit(solution)/shard_map/ppermute | solution.py:350

commit v3 on v2

--- a/solution.py
+++ b/solution.py
@@ -7,6 +7,7 @@
 from jax.experimental import pallas as pl
 from jax.experimental.pallas import tpu as pltpu
 from jax.sharding import PartitionSpec as P
+
 
 rate_year = 0.05
 step_years = 0.1
@@ -134,19 +135,23 @@
     return with_norm((t1, t2, t1, t3, t2, t1), -half, 3)
 
 
-def build_sources(states_ref, columns_ref, left_ref):
+def build_sources(states_refs, columns_ref, left_ref):
     inverse, drift_term = columns_ref[0], columns_ref[1]
     assets = inverse.shape[0]
+    slabs = left_ref.shape[0] // lanes // len(states_refs)
     for slab in range(left_ref.shape[0] // lanes):
-        states = states_ref[slab * assets : (slab + 1) * assets, :]
+        row = slab % slabs * assets
+        states = states_refs[slab // slabs][row : row + assets, :]
         left_ref[slab * lanes : (slab + 1) * lanes, :] = source_operand(states, inverse, drift_term)
 
 
-def build_sinks(states_ref, start, columns_ref, right_ref):
+def build_sinks(states_refs, start, columns_ref, right_ref):
     inverse = columns_ref[0]
     assets = inverse.shape[0]
+    slabs = right_ref.shape[1] // lanes // len(states_refs)
     for slab in range(right_ref.shape[1] // lanes):
-        states = states_ref[start + slab * assets : start + (slab + 1) * assets, :]
+        row = start + slab % slabs * assets
+        states = states_refs[slab // slabs][row : row + assets, :]
         right_ref[:, slab * lanes : (slab + 1) * lanes] = sink_operand(states, inverse)
 
 
@@ -181,10 +186,9 @@
         row += height
 
 
-def side_kernel(table_ref, packed_ref, columns_ref, payoff_ref):
+def columns_kernel(table_ref, packed_ref, columns_ref):
     dates, assets = table_ref.shape[0] - 1, table_ref.shape[1]
     index = table_ref[dates : dates + 1, 0:1]
-    strike = table_ref[dates : dates + 1, 1:2]
     rows = lax.broadcasted_iota(jnp.int32, (dates, assets), 0).astype(jnp.float32)
     vol_row = jnp.sum(
         jnp.where(rows == index, table_ref[0:dates, :], 0.0), axis=0, keepdims=True
@@ -199,27 +203,33 @@
     vol = jnp.broadcast_to(vol, (assets, lanes))
     columns_ref[0] = 1.0 / (vol * math.sqrt(step_years))
     columns_ref[1] = (rate_year - 0.5 * vol * vol) * step_years
+
+
+def payoff_kernel(table_ref, packed_ref, payoff_ref):
+    assets = table_ref.shape[1]
+    strike = table_ref[table_ref.shape[0] - 1 :, 1:2]
     for slab in range(payoff_ref.shape[0]):
         prices = jnp.exp(packed_ref[slab * assets : (slab + 1) * assets, :])
         best = jnp.max(prices, axis=0, keepdims=True)
         payoff_ref[slab : slab + 1, :] = jnp.maximum(best - strike, 0.0)
 
 
-def column_kernel(sources, columns_ref, packed_ref, left_ref, right_ref, density_ref):
-    build_sources(packed_ref, columns_ref, left_ref)
-    build_sinks(packed_ref, sources, columns_ref, right_ref)
+def near_kernel(sources, columns_ref, first_ref, second_ref, left_ref, right_ref, density_ref):
+    build_sources((first_ref, second_ref), columns_ref, left_ref)
+    build_sinks((first_ref, second_ref), sources, columns_ref, right_ref)
     add_density((left_ref,), right_ref, density_ref, 0, None)
 
 
-def column_other_kernel(columns_ref, other_ref, left_ref, right_ref, density_ref):
-    build_sinks(other_ref, 0, columns_ref, right_ref)
+def near_other_kernel(columns_ref, other_ref, left_ref, right_ref, density_ref):
+    build_sinks((other_ref,), 0, columns_ref, right_ref)
     add_density((left_ref,), right_ref, density_ref, 0, None)
 
 
 def far_kernel(
     sources,
     columns_ref,
-    packed_ref,
+    first_ref,
+    second_ref,
     left_ref,
     right_ref,
     base_ref,
@@ -227,8 +237,8 @@
     far_right_ref,
     density_ref,
 ):
-    build_sources(packed_ref, columns_ref, far_left_ref)
-    build_sinks(packed_ref, sources, columns_ref, far_right_ref)
+    build_sources((first_ref, second_ref), columns_ref, far_left_ref)
+    build_sinks((first_ref, second_ref), sources, columns_ref, far_right_ref)
     add_density((far_left_ref,), right_ref, density_ref, 0, base_ref)
     add_density((left_ref, far_left_ref), far_right_ref, density_ref, base_ref.shape[0], None)
 
@@ -243,7 +253,7 @@
     far_right_ref,
     density_ref,
 ):
-    build_sinks(other_ref, 0, columns_ref, far_right_ref)
+    build_sinks((other_ref,), 0, columns_ref, far_right_ref)
     add_density((far_left_ref,), right_ref, density_ref, 0, base_ref)
     add_density((left_ref, far_left_ref), far_right_ref, density_ref, base_ref.shape[0], None)
 
@@ -264,23 +274,10 @@
             place += width
 
 
-def weight_kernel(
-    values_start,
-    matrix_ref,
-    density_ref,
-    received_ref,
-    packed_ref,
-    far_packed_ref,
-    other_ref,
-    far_other_ref,
-    payoff_ref,
-    continuation_ref,
-    node_ref,
-    ratio_ref,
-):
+def weight_kernel(matrix_ref, density_ref, received_ref, *refs):
+    *values_refs, payoff_ref, continuation_ref, node_ref, ratio_ref = refs
     slabs = density_ref.shape[0]
     half = slabs // 2
-    quarter = half // 2
     inverse = 1.0 / jnp.concatenate(
         [
             density_ref[:half, :] + received_ref[half:, :],
@@ -289,17 +286,14 @@
         axis=0,
     )
     ratio_ref[1] = inverse
-    other_start = other_ref.shape[0] - quarter
-    for k, (values_ref, start) in enumerate(
-        (
-            (packed_ref, values_start),
-            (far_packed_ref, values_start),
-            (other_ref, other_start),
-            (far_other_ref, other_start),
-        )
-    ):
-        part = slice(k * quarter, (k + 1) * quarter)
-        ratio_ref[0, part, :] = values_ref[start : start + quarter, :] * inverse[part]
+    assets_twice = 2 * (values_refs[-1].shape[0] // (slabs // 4) - 1)
+    row = 0
+    for k, values_ref in enumerate(values_refs):
+        rows_per_slab = assets_twice + 1 if k < 4 else assets_twice // 2 + 1
+        count = values_ref.shape[0] // rows_per_slab
+        values = values_ref[values_ref.shape[0] - count :, :]
+        ratio_ref[0, row : row + count, :] = values * inverse[row : row + count]
+        row += count
     count = matrix_ref.shape[0]
     height = math.gcd(count, 64)
     sums = []
@@ -326,7 +320,7 @@
 vmem = pl.BlockSpec(memory_space=pltpu.VMEM)
 
 
-def local_call(kernel, name, in_specs, out_shapes, matmul_pairs=0, scratch_shapes=()):
+def local_call(kernel, in_specs, out_shapes, matmul_pairs=0, scratch_shapes=()):
     cost = pl.CostEstimate(
         flops=2 * depth * matmul_pairs, transcendentals=matmul_pairs, bytes_accessed=0
     )
@@ -338,7 +332,6 @@
         scratch_shapes=scratch_shapes,
         cost_estimate=cost,
         compiler_params=pltpu.CompilerParams(vmem_limit_bytes=vmem_grant),
-        name=name,
     )
 
 
@@ -366,59 +359,57 @@
     tile_rows = lax.broadcasted_iota(jnp.int32, rows.shape, 0)
     pieces.append(jnp.where(tile_rows < own_slabs, rows, pieces[0]))
     (packed,) = local_call(
-        pack_kernel,
-        "pack",
-        [vmem] * len(pieces),
-        [floats((2 * assets + 1) * own_slabs, lanes)],
+        pack_kernel, [vmem] * len(pieces), [floats((2 * assets + 1) * own_slabs, lanes)]
     )(*pieces)
     places = lax.broadcasted_iota(jnp.int32, (1, assets), 1)
     last = jnp.where(places == 0, date_index.astype(jnp.float32), jnp.where(places == 1, strike, 0.0))
     table = jnp.concatenate([vol_table, last], axis=0)
-    columns, payoff = local_call(
-        side_kernel, "side", [vmem, vmem], [floats(2, assets, lanes), floats(own_slabs, lanes)]
-    )(table, packed)
+    (columns,) = local_call(columns_kernel, [vmem, vmem], [floats(2, assets, lanes)])(table, packed)
 
     slabs = own_slabs
     mask = blk_size // 2
-    while mask > 2:
+    while mask > 4:
         received = across(packed, mask)
         cuts = (0, assets * slabs, 2 * assets * slabs, (2 * assets + 1) * slabs)
         packed = jnp.concatenate(
             [part[a:b] for a, b in zip(cuts, cuts[1:]) for part in (packed, received)], axis=0
         )
         if slabs == own_slabs:
-            packed, columns, payoff = lax.optimization_barrier((packed, columns, payoff))
+            packed, columns = lax.optimization_barrier((packed, columns))
         slabs *= 2
         mask //= 2
     sources = assets * slabs
+    near = across(packed, 2)
+    far_first = across(packed, 6)
+    far_second = across(packed, 4)
+
+    (payoff,) = local_call(payoff_kernel, [vmem, vmem], [floats(own_slabs, lanes)])(table, packed)
+
+    def sinks(first, second):
+        targets, values = slice(sources, 2 * sources), slice(2 * sources, None)
+        return jnp.concatenate([first[targets], second[targets], first[values], second[values]])
+
+    slabs *= 2
     nodes = slabs * lanes
-    far = across(packed, 2)
-    other = across(packed[sources:], 1)
+    near_other = across(sinks(packed, near), 1)
     left, right, base = local_call(
-        functools.partial(column_kernel, sources),
-        "column",
-        [vmem, vmem],
+        functools.partial(near_kernel, sources),
+        [vmem] * 3,
         [halves(nodes, depth), halves(depth, nodes), floats(slabs, lanes)],
         nodes * nodes,
-    )(columns, packed)
+    )(columns, packed, near)
     other_right, other_base = local_call(
-        column_other_kernel,
-        "column_other",
-        [vmem] * 3,
-        [halves(depth, nodes), floats(slabs, lanes)],
-        nodes * nodes,
-    )(columns, other, left)
-    far_other = across(far[sources:], 1)
+        near_other_kernel, [vmem] * 3, [halves(depth, nodes), floats(slabs, lanes)], nodes * nodes
+    )(columns, near_other, left)
+    far_other = across(sinks(far_first, far_second), 1)
     far_left, far_right, density = local_call(
         functools.partial(far_kernel, sources),
-        "far",
-        [vmem] * 5,
+        [vmem] * 6,
         [halves(nodes, depth), halves(depth, nodes), floats(2 * slabs, lanes)],
         3 * nodes * nodes,
-    )(columns, far, left, right, base)
+    )(columns, far_first, far_second, left, right, base)
     far_other_right, other_density = local_call(
         far_other_kernel,
-        "far_other",
         [vmem] * 6,
         [halves(depth, nodes), floats(2 * slabs, lanes)],
         3 * nodes * nodes,
@@ -426,15 +417,25 @@
     density = jnp.concatenate([density, other_density], axis=0)
     received = across(density, 1)
     (matrix,) = local_call(
-        matrix_kernel, "matrix", [vmem] * 5, [floats(count, 4 * nodes)], 4 * count * nodes
+        matrix_kernel, [vmem] * 5, [floats(count, 4 * nodes)], 4 * count * nodes
     )(left[:count], right, far_right, other_right, far_other_right)
     continuation, node_value = local_call(
-        functools.partial(weight_kernel, 2 * sources),
-        "weights",
-        [vmem] * 8,
+        weight_kernel,
+        [vmem] * 10,
         [floats(own_slabs, lanes)] * 2,
         scratch_shapes=[pltpu.VMEM((2, 4 * slabs, lanes), jnp.float32)],
-    )(matrix, density, received, packed, far, other, far_other, payoff)
+    )(
+        matrix,
+        density,
+        received,
+        packed,
+        near,
+        far_first,
+        far_second,
+        near_other,
+        far_other,
+        payoff,
+    )
     return continuation.reshape(count), node_value.reshape(count)
 
 

time: 24.2 us -> 23.7 us (0.979)
  waiting for transfers between devices: 4.78 us -> 3.95 us
  starting transfers between devices: 8.07 us -> 8.37 us
    ppermute x6 -> x7, waiting for transfers between devices: 4.78 us -> 3.95 us  [across(): return lax.ppermute(array, 'blk', [(i, i ^ mask) for i in range(blk_size)])]
    ppermute x6 -> x7, starting transfers between devices: 8.07 us -> 8.37 us  [across(): return lax.ppermute(array, 'blk', [(i, i ^ mask) for i in range(blk_size)])]
    pallas_call x8 -> x9, Pallas kernels: 7.39 us -> 7.48 us  [the longest x1 1.86 us: doubled_body(): local_call(functools.partial(far_kernel, sources), [vmem] * 6, [halves(no...]
  transfers between devices with their start and end apart: 6 -> 7, of which waited for: 5 -> 5; matrix products, arithmetic and copies ran while one was open for 3% -> 3% of each run, Pallas kernels for 18% -> 18%
where the time goes in v3:
time: 23.7 us; the launch traced here: 23.5 us
  starting transfers between devices  8.37 us (35%)
  Pallas kernels  7.48 us (32%)
  waiting for transfers between devices  3.95 us (17%)
  between operations  2.06 us (9%)
  other arithmetic  1.58 us (7%)
    ppermute x7, starting transfers between devices, across(): return lax.ppermute(array, 'blk', [(i, i ^ mask) for i in range(blk_size)])  8.37 us
    ppermute x7, waiting for transfers between devices, across(): return lax.ppermute(array, 'blk', [(i, i ^ mask) for i in range(blk_size)])  3.95 us
    pallas_call x1, Pallas kernels, doubled_body(): local_call(functools.partial(far_kernel, sources), [vmem] * 6, [halves(no...  1.86 us
    pallas_call x1, Pallas kernels, doubled_body(): local_call(far_other_kernel, [vmem] * 6, [halves(depth, nodes), floats(2...  1.79 us
    pallas_call x1, Pallas kernels, doubled_body(): local_call(weight_kernel, [vmem] * 10, [floats(own_slabs, lanes)] * 2, sc...  1.42 us
    select_n x1, other arithmetic, doubled_body(): pieces.append(jnp.where(tile_rows < own_slabs, rows, pieces[0]))  0.84 us
    pallas_call x1, Pallas kernels, doubled_body(): local_call(functools.partial(near_kernel, sources), [vmem] * 3, [halves(n...  0.78 us
    pallas_call x1, Pallas kernels, doubled_body(): local_call(near_other_kernel, [vmem] * 3, [halves(depth, nodes), floats(s...  0.74 us
  transfers between devices with their start and end apart: 7, of which 5 were waited for; matrix products, arithmetic and copies ran while one was open for 3% of the time, Pallas kernels for 18%

profile of v3, /device:TPU:0, one launch (start us, length us, event | category | flops | bytes accessed | tf_op | source)
XLA Modules:
  0.0 23.5 jit_solution(4398254142417869677)
XLA Ops:
  0.6 0.8 %pad_select_fusion = (f32[16,128]{1,0:T(8,128)S(1)}, f32[16,128]{1,0:T(8,128)S(1)}, f32[16,128]{1,0:T(8,128)S(1)}, f32[16,128]{1,0:T(8,128)S(1)}, f32[16,128]{1,0:T(8,128)S(1)}) fusion(f32[2,128]{1,0:T(2,128)} %bitcast.6, pred[16]{0:T(512)(128)(4,1)S(1)} %iota_compare_fusion, f32[16,256]{1,0:T(8,128)} %param.6, f32[16,256]{1,0:T(8,128)} %param.7), kind=kLoop, calls=%fused_computation.3 | loop fusion | flops 2048 | bytes 74768 | tf_op jit(solution)/shard_map/jit(_where)/select_n | solution.py:360
  1.5 4.1 %collective-permute-start = (f32[66,128]{1,0:T(8,128)S(1)}, f32[66,128]{1,0:T(8,128)S(1)}, u32[]{:S(2)}, u32[]{:S(2)}) collective-permute-start(f32[66,128]{1,0:T(8,128)S(1)} %shard_map.77.packed_ref), channel_id=1, source_target_pairs={{0,8},{1,9},{2,10},{3,11},{4,12},{5,13},{6,14},{7,15},{8,0},{9,1},... | collective-permute-start | bytes 101384 | tf_op jit(solution)/shard_map/ppermute | solution.py:343
  6.9 0.7 %pad_maximum_fusion.2.table_ref = f32[13,16]{1,0:T(8,128)S(1)} fusion(f32[1,16]{1,0:T(1,128)S(1)} %compare_select_fusion.1, f32[12,16]{1,0:T(8,128)} %param.9), kind=kLoop, calls=%fused_computation.2 | loop fusion | flops 208 | bytes 1664 | tf_op jit(solution)/shard_map/concatenate | solution.py:366
  7.6 0.1 shard_map.78.columns_ref
  7.8 0.2 collective-permute-done
  8.0 1.8 %collective-permute-start.1 = (f32[132,128]{1,0:T(8,128)S(1)}, f32[132,128]{1,0:T(8,128)S(1)}, u32[]{:S(2)}, u32[]{:S(2)}) collective-permute-start(f32[132,128]{1,0:T(8,128)S(1)} %concatenate.15.first_ref.packed_ref.refs_0_), channel_id=1, source_target_pairs={{0,2},{1,3},{2,0},{3,1},{4,6},{5,7},{6,4},{7,5},{8,10},{9,11},{10,... | collective-permute-start | bytes 202760 | tf_op jit(solution)/shard_map/ppermute | solution.py:343
  9.7 1.3 %collective-permute-start.2 = (f32[132,128]{1,0:T(8,128)S(1)}, f32[132,128]{1,0:T(8,128)S(1)}, u32[]{:S(2)}, u32[]{:S(2)}) collective-permute-start(f32[132,128]{1,0:T(8,128)S(1)} %concatenate.15.first_ref.packed_ref.refs_0_), channel_id=1, source_target_pairs={{0,6},{1,7},{2,4},{3,5},{4,2},{5,3},{6,0},{7,1},{8,14},{9,15},{10,... | collective-permute-start | bytes 202760 | tf_op jit(solution)/shard_map/ppermute | solution.py:343
  11.0 0.5 %collective-permute-start.3 = (f32[132,128]{1,0:T(8,128)S(1)}, f32[132,128]{1,0:T(8,128)S(1)}, u32[]{:S(2)}, u32[]{:S(2)}) collective-permute-start(f32[132,128]{1,0:T(8,128)S(1)} %concatenate.15.first_ref.packed_ref.refs_0_), channel_id=1, source_target_pairs={{0,4},{1,5},{2,6},{3,7},{4,0},{5,1},{6,2},{7,3},{8,12},{9,13},{10,... | collective-permute-start | bytes 202760 | tf_op jit(solution)/shard_map/ppermute | solution.py:343
  11.5 0.1 shard_map.84.refs_6_
  11.6 1.5 %collective-permute-done.1.second_ref.refs_1_ = f32[132,128]{1,0:T(8,128)S(1)} collective-permute-done((f32[132,128]{1,0:T(8,128)S(1)}, f32[132,128]{1,0:T(8,128)S(1)}, u32[]{:S(2)}, u32[]{:S(2)}) %collective-permute-start.1) | collective-permute-done | bytes 67616 | tf_op jit(solution)/shard_map/ppermute | solution.py:343
  13.1 0.1 collective-permute-start.4
  13.2 1.8 %collective-permute-done.2.first_ref.refs_2_ = f32[132,128]{1,0:T(8,128)S(1)} collective-permute-done((f32[132,128]{1,0:T(8,128)S(1)}, f32[132,128]{1,0:T(8,128)S(1)}, u32[]{:S(2)}, u32[]{:S(2)}) %collective-permute-start.2) | collective-permute-done | bytes 67616 | tf_op jit(solution)/shard_map/ppermute | solution.py:343
  15.0 0.4 %collective-permute-done.3.second_ref.refs_3_ = f32[132,128]{1,0:T(8,128)S(1)} collective-permute-done((f32[132,128]{1,0:T(8,128)S(1)}, f32[132,128]{1,0:T(8,128)S(1)}, u32[]{:S(2)}, u32[]{:S(2)}) %collective-permute-start.3) | collective-permute-done | bytes 67616 | tf_op jit(solution)/shard_map/ppermute | solution.py:343
  15.3 0.1 collective-permute-start.5
  15.4 0.8 %shard_map.79 = (bf16[1024,128]{1,0:T(8,128)(2,1)S(1)}, bf16[128,1024]{1,0:T(8,128)(2,1)S(1)}, f32[8,128]{1,0:T(8,128)S(1)}) custom-call(f32[2,16,128]{2,1,0:T(8,128)S(1)} %shard_map.78.columns_ref, f32[132,128]{1,0:T(8,128)S(1)} %concatenate.15.first_ref.packed_ref.refs_0_, f32[132,128]{1,0:T(8,128)S(1)} %collective-permute-done.1.second_ref.refs_1_), custom_call_target="tpu_custom_call" | custom-call | flops 268435456 | tf_op jit(solution)/shard_map/pallas_call | solution.py:395
  16.2 1.9 %shard_map.80 = (bf16[1024,128]{1,0:T(8,128)(2,1)S(1)}, bf16[128,1024]{1,0:T(8,128)(2,1)S(1)}, f32[16,128]{1,0:T(8,128)S(1)}) custom-call(f32[2,16,128]{2,1,0:T(8,128)S(1)} %shard_map.78.columns_ref, f32[132,128]{1,0:T(8,128)S(1)} %collective-permute-done.2.first_ref.refs_2_, f32[132,128]{1,0:T(8,128)S(1)} %collective-permute-done.3.second_ref.refs_3_, ...), custom_call_target="tpu_custom_call" | custom-call | flops 805306368 | tf_op jit(solution)/shard_map/pallas_call | solution.py:405
  18.1 0.0 collective-permute-done.4.other_ref.refs_4_
  18.1 0.7 %shard_map.81 = (bf16[128,1024]{1,0:T(8,128)(2,1)S(1)}, f32[8,128]{1,0:T(8,128)S(1)}) custom-call(f32[2,16,128]{2,1,0:T(8,128)S(1)} %shard_map.78.columns_ref, f32[136,128]{1,0:T(8,128)S(1)} %collective-permute-done.4.other_ref.refs_4_, bf16[1024,128]{1,0:T(8,128)(2,1)S(1)} %get-tuple-element.18.left_ref), custom_call_target="tpu_custom_call" | custom-call | flops 268435456 | tf_op jit(solution)/shard_map/pallas_call | solution.py:401
  18.9 0.0 collective-permute-done.5.other_ref.refs_5_
  18.9 1.8 %shard_map.82 = (bf16[128,1024]{1,0:T(8,128)(2,1)S(1)}, f32[16,128]{1,0:T(8,128)S(1)}) custom-call(f32[2,16,128]{2,1,0:T(8,128)S(1)} %shard_map.78.columns_ref, f32[136,128]{1,0:T(8,128)S(1)} %collective-permute-done.5.other_ref.refs_5_, bf16[1024,128]{1,0:T(8,128)(2,1)S(1)} %get-tuple-element.18.left_ref, ...), custom_call_target="tpu_custom_call" | custom-call | flops 805306368 | tf_op jit(solution)/shard_map/pallas_call | solution.py:411
  20.7 0.6 %collective-permute-start.6 = (f32[32,128]{1,0:T(8,128)S(1)}, f32[32,128]{1,0:T(8,128)S(1)}, u32[]{:S(2)}, u32[]{:S(2)}) collective-permute-start(f32[32,128]{1,0:T(8,128)S(1)} %constant_dynamic-update-slice_fusion.density_ref), channel_id=1, source_target_pairs={{0,1},{1,0},{2,3},{3,2},{4,5},{5,4},{6,7},{7,6},{8,9},{9,8},{10,11... | collective-permute-start | bytes 49160 | tf_op jit(solution)/shard_map/ppermute | solution.py:343
  21.2 0.7 %shard_map.83.matrix_ref = f32[256,4096]{1,0:T(8,128)S(1)} custom-call(bf16[256,128]{1,0:T(8,128)(2,1)S(1)} %slice.67.left_ref, bf16[128,1024]{1,0:T(8,128)(2,1)S(1)} %get-tuple-element.19.right_ref.refs_0_, bf16[128,1024]{1,0:T(8,128)(2,1)S(1)} %get-tuple-element.21.refs_1_, bf16[128,1024]{1,0:T(8,128)(2,1)S(1)} %get-tuple-element.22.right_ref.refs_2_, ...), custom_call_target="tpu_custom_call" | custom-call | flops 268435456 | tf_op jit(solution)/shard_map/pallas_call | solution.py:419
  21.9 0.1 collective-permute-done.6.received_ref
  22.1 1.4 %shard_map.85 = (f32[2,128]{1,0:T(2,128)}, f32[2,128]{1,0:T(2,128)}) custom-call(f32[256,4096]{1,0:T(8,128)S(1)} %shard_map.83.matrix_ref, f32[32,128]{1,0:T(8,128)S(1)} %constant_dynamic-update-slice_fusion.density_ref, f32[32,128]{1,0:T(8,128)S(1)} %collective-permute-done.6.received_ref, f32[132,128]{1,0:T(8,128)S(1)} %concatenate.15.first_ref.packed_ref.refs_0_, ...), custom_call_target="tpu_custom_call" | custom-call | tf_op jit(solution)/shard_map/pallas_call | solution.py:422
  (21 shorter events, 0.1 us)
Async XLA Ops:
  1.5 6.5 %collective-permute-start = (f32[66,128]{1,0:T(8,128)S(1)}, f32[66,128]{1,0:T(8,128)S(1)}, u32[]{:S(2)}, u32[]{:S(2)}) collective-permute-start(f32[66,128]{1,0:T(8,128)S(1)} %shard_map.77.packed_ref), channel_id=1, source_target_pairs={{0,8},{1,9},{2,10},{3,11},{4,12},{5,13},{6,14},{7,15},{8,0},{9,1},... | collective-permute-start | bytes 101384 | tf_op jit(solution)/shard_map/ppermute | solution.py:343
  8.0 5.1 %collective-permute-start.1 = (f32[132,128]{1,0:T(8,128)S(1)}, f32[132,128]{1,0:T(8,128)S(1)}, u32[]{:S(2)}, u32[]{:S(2)}) collective-permute-start(f32[132,128]{1,0:T(8,128)S(1)} %concatenate.15.first_ref.packed_ref.refs_0_), channel_id=1, source_target_pairs={{0,2},{1,3},{2,0},{3,1},{4,6},{5,7},{6,4},{7,5},{8,10},{9,11},{10,... | collective-permute-start | bytes 202760 | tf_op jit(solution)/shard_map/ppermute | solution.py:343
  9.7 5.2 %collective-permute-start.2 = (f32[132,128]{1,0:T(8,128)S(1)}, f32[132,128]{1,0:T(8,128)S(1)}, u32[]{:S(2)}, u32[]{:S(2)}) collective-permute-start(f32[132,128]{1,0:T(8,128)S(1)} %concatenate.15.first_ref.packed_ref.refs_0_), channel_id=1, source_target_pairs={{0,6},{1,7},{2,4},{3,5},{4,2},{5,3},{6,0},{7,1},{8,14},{9,15},{10,... | collective-permute-start | bytes 202760 | tf_op jit(solution)/shard_map/ppermute | solution.py:343
  11.0 4.3 %collective-permute-start.3 = (f32[132,128]{1,0:T(8,128)S(1)}, f32[132,128]{1,0:T(8,128)S(1)}, u32[]{:S(2)}, u32[]{:S(2)}) collective-permute-start(f32[132,128]{1,0:T(8,128)S(1)} %concatenate.15.first_ref.packed_ref.refs_0_), channel_id=1, source_target_pairs={{0,4},{1,5},{2,6},{3,7},{4,0},{5,1},{6,2},{7,3},{8,12},{9,13},{10,... | collective-permute-start | bytes 202760 | tf_op jit(solution)/shard_map/ppermute | solution.py:343
  13.1 5.0 %collective-permute-start.4 = (f32[136,128]{1,0:T(8,128)S(1)}, f32[136,128]{1,0:T(8,128)S(1)}, u32[]{:S(2)}, u32[]{:S(2)}) collective-permute-start(f32[136,128]{1,0:T(8,128)S(1)} %pad_maximum_fusion), channel_id=1, source_target_pairs={{0,1},{1,0},{2,3},{3,2},{4,5},{5,4},{6,7},{7,6},{8,9},{9,8},{10,11... | collective-permute-start | bytes 208904 | tf_op jit(solution)/shard_map/ppermute | solution.py:343
  15.3 3.5 %collective-permute-start.5 = (f32[136,128]{1,0:T(8,128)S(1)}, f32[136,128]{1,0:T(8,128)S(1)}, u32[]{:S(2)}, u32[]{:S(2)}) collective-permute-start(f32[136,128]{1,0:T(8,128)S(1)} %pad_maximum_fusion.1), channel_id=1, source_target_pairs={{0,1},{1,0},{2,3},{3,2},{4,5},{5,4},{6,7},{7,6},{8,9},{9,8},{10,11... | collective-permute-start | bytes 208904 | tf_op jit(solution)/shard_map/ppermute | solution.py:343
  20.7 1.4 %collective-permute-start.6 = (f32[32,128]{1,0:T(8,128)S(1)}, f32[32,128]{1,0:T(8,128)S(1)}, u32[]{:S(2)}, u32[]{:S(2)}) collective-permute-start(f32[32,128]{1,0:T(8,128)S(1)} %constant_dynamic-update-slice_fusion.density_ref), channel_id=1, source_target_pairs={{0,1},{1,0},{2,3},{3,2},{4,5},{5,4},{6,7},{7,6},{8,9},{9,8},{10,11... | collective-permute-start | bytes 49160 | tf_op jit(solution)/shard_map/ppermute | solution.py:343
